TPU v7x, 32 devices: a whole 2x2x4 slice. The times are simulated.
32 devices in a mesh: traj: 8 (over z, core), amp: 4 (over y, x).
Axes of the slice: x: 2, y: 2, z: 4, core: 2. Of those that a mesh axis runs over, the one named last changes fastest.
Arguments:
- amplitudes: float32 [8, 2, 524288], P('traj', None, 'amp'), parts along dimension 0, may hold values from -6 to 6
- couplings: float32 [18], replicated, may hold values from 0.5 to 2
- fields: float32 [19], replicated, may hold values from 0.5 to 2
- decays: float32 [19], replicated, may hold values from 0.2 to 2
- channel: int32 [8], P('traj'), parts along dimension 0, may hold values from 0 to 19
Outputs:
- evolved_state: float32 [8, 2, 524288], P('traj', None, 'amp'), parts along dimension 0
There are 8 independent parts, one for each index of `traj`. A program takes and returns all parts, laid end to end along the dimension named above; an argument that names none is the same for every part. Nothing has to cross between parts.
Inputs may be any that keep to these rules, and one draw needn't show every extreme that they name: `channel`: the value 19 means that the trajectory does not jump.
All inputs are finite; a program needn't handle non-finite values.
Results may differ from a plain program's by a relative error of at most 0.0003.
Values sent between devices are 32-bit elements; how exact they have to be, the bound alone decides.
A program may use at most 256 MiB of HBM per device.

v0:
```python
import jax
import jax.numpy as jnp
from jax import lax
from jax.experimental import pallas as pl
from jax.experimental.pallas import tpu as pltpu
from jax.sharding import PartitionSpec as P

SPINS = 19
KRYLOV = 8
LANES = 128
LANE_BITS = 7

time_step = 0.7
squarings = 8
taylor_order = 10
highest = lax.Precision.HIGHEST

CHUNK_BITS = 8
CHUNK = 1 << CHUNK_BITS
SUB = 32


def split(x):
    hi = x.astype(jnp.bfloat16)
    lo = (x - hi.astype(jnp.float32)).astype(jnp.bfloat16)
    return hi, lo


def dot(a, b):
    return jnp.dot(a, b, preferred_element_type=jnp.float32)


def fold(x):
    return jnp.sum(x.reshape(x.shape[0] // 8, 8, x.shape[1]), axis=0)


def scalar_sqrt(value):
    root = jnp.sqrt(jnp.full((8, LANES), value, jnp.float32))
    return jnp.max(root), jnp.max(1.0 / root)


def krylov_weights(a_matrix):
    size = a_matrix.shape[0]
    pad = jnp.zeros((LANES - size, LANES), jnp.float32)
    scaled = jnp.concatenate([a_matrix, pad], axis=0) * (1.0 / 2.0**squarings)
    rows = lax.broadcasted_iota(jnp.int32, (LANES, LANES), 0)
    cols = lax.broadcasted_iota(jnp.int32, (LANES, LANES), 1)
    identity = jnp.where(rows == cols, 1.0, 0.0).astype(jnp.float32)
    series = identity
    for degree in range(taylor_order, 0, -1):
        product = jnp.dot(
            scaled, series, precision=highest, preferred_element_type=jnp.float32
        )
        series = identity + product * (1.0 / degree)
    for repeat in range(squarings):
        series = jnp.dot(
            series, series, precision=highest, preferred_element_type=jnp.float32
        )
    return series


def kernel(
    channel_ref,
    couplings,
    fields,
    decays,
    state,
    out,
    basis,
    work,
    flips,
    row_table,
    lane_table,
    diag_low,
):
    node_count, _, block_rows, _ = state.shape
    rows = node_count * block_rows
    chunks = rows // CHUNK
    subs = CHUNK // SUB
    channel = channel_ref[0]
    device = lax.axis_index("amp")
    zero_tile = jnp.zeros((8, LANES), jnp.float32)
    per_block = block_rows // CHUNK

    table_shape = (CHUNK, CHUNK)
    crossed = lax.broadcasted_iota(jnp.int32, table_shape, 0)
    crossed = crossed ^ lax.broadcasted_iota(jnp.int32, table_shape, 1)
    for table, first_spin, bits in (
        (row_table, LANE_BITS, CHUNK_BITS),
        (lane_table, 0, LANE_BITS),
    ):
        value = jnp.zeros(table_shape, jnp.float32)
        for bit in range(bits):
            value = jnp.where(crossed == 1 << bit, fields[first_spin + bit], value)
        table[0], table[1] = split(value)

    low_shape = (CHUNK, LANES)
    low_pos = lax.broadcasted_iota(jnp.int32, low_shape, 0) * LANES
    low_pos = low_pos + lax.broadcasted_iota(jnp.int32, low_shape, 1)
    low_bits = LANE_BITS + CHUNK_BITS
    before = None
    low_real = jnp.zeros(low_shape, jnp.float32)
    low_imag = jnp.zeros(low_shape, jnp.float32)
    for spin in range(low_bits):
        occupied = (lax.shift_right_logical(low_pos, spin) & 1).astype(jnp.float32)
        sign = 1.0 - 2.0 * occupied
        low_imag = low_imag - 0.5 * decays[spin] * occupied
        if spin > 0:
            low_real = low_real - couplings[spin - 1] * (before * sign)
        before = sign
    diag_low[0] = low_real
    diag_low[1] = low_imag

    def high_diagonal(i):
        bits = [
            (lax.shift_right_logical(i, b) & 1).astype(jnp.float32)
            for b in range(SPINS - low_bits)
        ]
        signs = [1.0 - 2.0 * bit for bit in bits]
        real = jnp.float32(0.0)
        imag = jnp.float32(0.0)
        for b in range(len(bits)):
            imag = imag - 0.5 * decays[low_bits + b] * bits[b]
            if b > 0:
                real = real - couplings[low_bits + b - 1] * signs[b - 1] * signs[b]
        edge = couplings[low_bits - 1] * signs[0]
        return real - edge, real + edge, imag

    def start_norm(i, acc):
        node = i // per_block
        first = (i % per_block) * CHUNK
        for part in range(2):
            x = state[node, part, pl.ds(first, CHUNK), :]
            acc = acc + fold(x * x)
        return acc

    start_sq = jnp.sum(lax.fori_loop(0, chunks, start_norm, zero_tile))
    beta, inv_beta = scalar_sqrt(start_sq)

    def start_vector(i, carry):
        node = i // per_block
        first = (i % per_block) * CHUNK
        for part in range(2):
            basis[0, pl.ds(i * CHUNK, CHUNK), part * LANES : (part + 1) * LANES] = (
                state[node, part, pl.ds(first, CHUNK), :] * inv_beta
            )
        return carry

    lax.fori_loop(0, chunks, start_vector, 0)

    mat_rows = lax.broadcasted_iota(jnp.int32, (2 * KRYLOV, LANES), 0)
    mat_cols = lax.broadcasted_iota(jnp.int32, (2 * KRYLOV, LANES), 1)
    a_matrix = jnp.zeros((2 * KRYLOV, LANES), jnp.float32)

    def put(matrix, k, j, real, imag):
        a_real = time_step * imag
        a_imag = -time_step * real
        for r, c, value in (
            (k, j, a_real),
            (k, j + KRYLOV, -a_imag),
            (k + KRYLOV, j, a_imag),
            (k + KRYLOV, j + KRYLOV, a_real),
        ):
            matrix = jnp.where((mat_rows == r) & (mat_cols == c), value, matrix)
        return matrix

    high_fields = [
        fields[LANE_BITS + CHUNK_BITS + b] for b in range(SPINS - LANE_BITS - CHUNK_BITS)
    ]

    for j in range(KRYLOV):
        last = j + 1 == KRYLOV

        def apply_chunk(i, acc, j=j):
            base = pl.multiple_of(i * CHUNK, CHUNK)
            hi, lo = split(basis[j, pl.ds(base, CHUNK), :])
            flips[...] = (
                dot(row_table[0], hi)
                + dot(row_table[1], hi)
                + dot(row_table[0], lo)
                + dot(hi, lane_table[0])
                + dot(lo, lane_table[0])
                + dot(hi, lane_table[1])
            )
            acc = list(acc)
            real_vacant, real_occupied, imag_high = high_diagonal(i)
            for s in range(subs):
                here = pl.ds(base + s * SUB, SUB)
                x = basis[j, here, :]
                f = flips[s * SUB : (s + 1) * SUB, :]
                for b, field in enumerate(high_fields):
                    there = pl.multiple_of((i ^ (1 << b)) * CHUNK, CHUNK)
                    f = f + field * basis[j, pl.ds(there + s * SUB, SUB), :]
                part = slice(s * SUB, (s + 1) * SUB)
                dr = diag_low[0, part, :] + (real_vacant if s < subs // 2 else real_occupied)
                di = diag_low[1, part, :] + imag_high
                xr, xi = x[:, :LANES], x[:, LANES:]
                wr = dr * xr - di * xi - f[:, :LANES]
                wi = dr * xi + di * xr - f[:, LANES:]
                work[here, :LANES] = wr
                work[here, LANES:] = wi
                for k in range(j + 1):
                    vr = basis[k, here, :LANES]
                    vi = basis[k, here, LANES:]
                    acc[2 * k] = acc[2 * k] + fold(vr * wr + vi * wi)
                    acc[2 * k + 1] = acc[2 * k + 1] + fold(vr * wi - vi * wr)
                acc[-1] = acc[-1] + fold(wr * wr + wi * wi)
            return tuple(acc)

        sums = lax.fori_loop(0, chunks, apply_chunk, (zero_tile,) * (2 * j + 3))
        coeffs = [jnp.sum(t) for t in sums]
        for k in range(j + 1):
            a_matrix = put(a_matrix, k, j, coeffs[2 * k], coeffs[2 * k + 1])
        if last:
            break
        left = coeffs[-1]
        for value in coeffs[:-1]:
            left = left - value * value
        norm, inv_norm = scalar_sqrt(left)
        a_matrix = put(a_matrix, j + 1, j, norm, jnp.float32(0.0))

        def subtract_chunk(i, carry, j=j, coeffs=coeffs, inv_norm=inv_norm):
            base = pl.multiple_of(i * CHUNK, CHUNK)
            for s in range(subs):
                here = pl.ds(base + s * SUB, SUB)
                rr = work[here, :LANES]
                ri = work[here, LANES:]
                for k in range(j + 1):
                    vr = basis[k, here, :LANES]
                    vi = basis[k, here, LANES:]
                    hr, hm = coeffs[2 * k], coeffs[2 * k + 1]
                    rr = rr - (hr * vr - hm * vi)
                    ri = ri - (hr * vi + hm * vr)
                basis[j + 1, here, :LANES] = rr * inv_norm
                basis[j + 1, here, LANES:] = ri * inv_norm
            return carry

        lax.fori_loop(0, chunks, subtract_chunk, 0)

    series = krylov_weights(a_matrix)
    first = series[: 2 * KRYLOV, :] * beta
    weights = [
        jnp.sum(jnp.where((mat_rows == k) & (mat_cols == 0), first, 0.0))
        for k in range(2 * KRYLOV)
    ]
    sub_pos = lax.broadcasted_iota(jnp.int32, (SUB, LANES), 0) * LANES
    sub_pos = sub_pos + lax.broadcasted_iota(jnp.int32, (SUB, LANES), 1)

    def combine(i, acc):
        base = pl.multiple_of(i * CHUNK, CHUNK)
        for s in range(subs):
            here = pl.ds(base + s * SUB, SUB)
            pr = jnp.zeros((SUB, LANES), jnp.float32)
            pi = jnp.zeros((SUB, LANES), jnp.float32)
            for k in range(KRYLOV):
                vr = basis[k, here, :LANES]
                vi = basis[k, here, LANES:]
                cr, ci = weights[k], weights[k + KRYLOV]
                pr = pr + (cr * vr - ci * vi)
                pi = pi + (cr * vi + ci * vr)
            work[here, :LANES] = pr
            work[here, LANES:] = pi
            position = sub_pos + (base + s * SUB) * LANES
            occupied = lax.shift_right_logical(position, channel) & 1
            acc = acc + fold(jnp.where(occupied == 1, pr * pr + pi * pi, 0.0))
        return acc

    total = jnp.sum(lax.fori_loop(0, chunks, combine, zero_tile))
    jumped = channel < SPINS
    size = jnp.float32(rows * LANES)
    total = jnp.where(jumped, total, size)
    root = jnp.sqrt(size / jnp.full((8, LANES), total, jnp.float32))
    scale = jnp.max(root)
    in_lanes = channel < LANE_BITS
    lane_shift = jnp.where(in_lanes, lax.shift_left(1, channel), 0)
    row_shift = jnp.where(
        in_lanes | (channel >= SPINS),
        0,
        lax.shift_left(1, jnp.maximum(channel - LANE_BITS, 0)),
    )
    in_sublanes = row_shift < 8
    near = jnp.where(in_sublanes, row_shift, 0)
    far = jnp.where(in_sublanes, 0, row_shift)
    lane_turn = (LANES - lane_shift) % LANES
    row_turn = (SUB - near) % SUB

    def jump(i, carry):
        local = pl.multiple_of(i * SUB, SUB)
        base = device * block_rows + local
        source = pl.multiple_of(base + far, 8)
        position = sub_pos + base * LANES
        vacant = (lax.shift_right_logical(position, channel) & 1) == 0
        for part in range(2):
            x = work[pl.ds(source, SUB), part * LANES : (part + 1) * LANES]
            x = pltpu.roll(x, row_turn, 0)
            x = pltpu.roll(x, lane_turn, 1)
            out[part, pl.ds(local, SUB), :] = jnp.where(vacant, x * scale, 0.0)
        return carry

    lax.fori_loop(0, block_rows // SUB, jump, 0)


def gather_kernel(block, out, send_sem, recv_sem):
    me = lax.axis_index("amp")
    near = (me ^ 1, me ^ 2)
    barrier = pltpu.get_barrier_semaphore()
    for partner in near:
        pl.semaphore_signal(
            barrier, inc=1, device_id={"amp": partner}, device_id_type=pl.DeviceIdType.MESH
        )
    pl.semaphore_wait(barrier, 2)

    def copy(source, owner, part, axis, slot):
        return pltpu.make_async_remote_copy(
            src_ref=source,
            dst_ref=out.at[owner, part],
            send_sem=send_sem.at[slot],
            recv_sem=recv_sem.at[slot],
            device_id={"amp": near[axis]},
            device_id_type=pl.DeviceIdType.MESH,
        )

    direct = {}
    for turn in range(2):
        for axis in range(2):
            part = axis ^ turn
            direct[axis, part] = copy(block.at[part], me, part, axis, 2 * axis + part)
            direct[axis, part].start()
    out[me] = block[...]
    forwards = []
    for axis in range(2):
        direct[axis, axis].wait_recv()
        owner = near[axis]
        forward = copy(out.at[owner, axis], owner, axis, 1 - axis, 4 + axis)
        forward.start()
        forwards.append(forward)
    for axis in range(2):
        direct[axis, 1 - axis].wait_recv()
    for forward in forwards:
        forward.wait_recv()
    for sent in list(direct.values()) + forwards:
        sent.wait_send()


def gather(block):
    node_count = lax.axis_size("amp")
    if node_count != 4:
        return lax.all_gather(block, "amp")
    vmem = pl.BlockSpec(memory_space=pltpu.VMEM)
    return pl.pallas_call(
        gather_kernel,
        out_shape=jax.ShapeDtypeStruct((node_count,) + block.shape, block.dtype),
        in_specs=[vmem],
        out_specs=vmem,
        scratch_shapes=[pltpu.SemaphoreType.DMA((6,)), pltpu.SemaphoreType.DMA((6,))],
        compiler_params=pltpu.CompilerParams(collective_id=0, has_side_effects=True),
        name="gather",
    )(block)


def body(amplitudes, couplings, fields, decays, channel):
    node_count = lax.axis_size("amp")
    local_len = amplitudes.shape[2]
    block_rows = local_len // LANES
    rows = node_count * block_rows
    vmem = pl.BlockSpec(memory_space=pltpu.VMEM)
    smem = pl.BlockSpec(memory_space=pltpu.SMEM)
    call = pl.pallas_call(
        kernel,
        out_shape=jax.ShapeDtypeStruct((2, block_rows, LANES), jnp.float32),
        in_specs=[smem] * 4 + [vmem],
        out_specs=vmem,
        scratch_shapes=[
            pltpu.VMEM((KRYLOV, rows, 2 * LANES), jnp.float32),
            pltpu.VMEM((rows + rows // 2, 2 * LANES), jnp.float32),
            pltpu.VMEM((CHUNK, 2 * LANES), jnp.float32),
            pltpu.VMEM((2, CHUNK, CHUNK), jnp.bfloat16),
            pltpu.VMEM((2, CHUNK, CHUNK), jnp.bfloat16),
            pltpu.VMEM((2, CHUNK, LANES), jnp.float32),
        ],
        compiler_params=pltpu.CompilerParams(vmem_limit_bytes=62 * 1024 * 1024),
        name="trajectory",
    )
    results = []
    for t in range(amplitudes.shape[0]):
        block = amplitudes[t].reshape(2, block_rows, LANES)
        state = gather(block)
        results.append(call(channel[t : t + 1], couplings, fields, decays, state))
    return jnp.stack(results).reshape(amplitudes.shape)


def solution(mesh):
    placed = (P("traj", None, "amp"), P(), P(), P(), P("traj"))
    return jax.shard_map(
        body, mesh=mesh, in_specs=placed, out_specs=P("traj", None, "amp"), check_vma=False
    )
```

profile of v0, /device:TPU:1, one launch (start us, length us, event | category | flops | bytes accessed | tf_op | source)
XLA Modules:
  0.0 159.5 jit_solution(3250776257495823717)
XLA Ops:
  0.7 2.3 %copy.8 = f32[1,2,1024,128]{3,2,1,0:T(8,128)} copy(f32[1,2,1024,128]{3,1,2,0:T(2,128)} %bitcast.6) | data formatting | bytes 2097152
  2.9 40.3 %gather.1.state = f32[4,2,1024,128]{3,2,1,0:T(8,128)} custom-call(f32[2,1024,128]{2,1,0:T(8,128)} %bitcast.5), custom_call_target="tpu_custom_call" | custom-call | tf_op jit(solution)/shard_map/gather/pallas_call | solution.py:350
  43.3 113.4 %trajectory.1 = f32[2,1024,128]{2,1,0:T(8,128)} custom-call(s32[1]{0:T(128)S(6)} %copy.9.channel_ref, f32[18]{0:T(128)} %couplings.1, f32[19]{0:T(128)} %fields.1, f32[19]{0:T(128)} %decays.1, f32[4,2,1024,128]{3,2,1,0:T(8,128)} %gather.1.state), custom_call_target="tpu_custom_call" | custom-call | tf_op jit(solution)/shard_map/trajectory/pallas_call | solution.py:388
  156.6 2.9 %reshape_stack.3 = f32[1,2,131072]{2,1,0:T(2,128)} reshape(f32[2,1024,128]{2,1,0:T(8,128)} %trajectory.1) | data formatting | bytes 2097152 | tf_op jit(solution)/shard_map/reshape;stack | solution.py:389
where the time goes:
time: 161 us; the launch traced here: 160 us
  Pallas kernels  154 us (96%)
  local copies, waits for them, and re-layouts  5.12 us (3%)
    pallas_call x1, Pallas kernels, body(): results.append(call(channel[t:t + 1], couplings, fields, decays, state))  113 us
    pallas_call x1, Pallas kernels, gather(): pl.pallas_call(gather_kernel, out_shape=jax.ShapeDtypeStruct((node_count,...  40.3 us

commit v1 on v0

--- a/solution.py
+++ b/solution.py
@@ -389,8 +389,549 @@
     return jnp.stack(results).reshape(amplitudes.shape)
 
 
+BLOCK = 256
+BLOCK_BITS = 8
+
+
+def pair_kernel(
+    channel_ref,
+    couplings,
+    fields,
+    decays,
+    block,
+    pieces,
+    scale_out,
+    landing,
+    basis,
+    work,
+    mate,
+    flips_even,
+    flips_odd,
+    row_table,
+    lane_table,
+    diag_low,
+    own_sums,
+    other_sums,
+    own_channel,
+    other_channel,
+    parcel,
+    gather_send,
+    gather_recv,
+    sums_send,
+    sums_recv,
+    mate_send,
+    mate_recv,
+    channel_sem,
+    parcel_send,
+    parcel_recv,
+    scale_sem,
+):
+    quarters = landing.shape[0]
+    piece_rows = landing.shape[1]
+    traj = lax.axis_index("traj")
+    me = lax.axis_index("amp")
+    core = traj & 1
+    first_traj = traj - core
+    held = (me ^ (me >> 1)) & 1
+    stays = core == held
+    split_spin = LANE_BITS + BLOCK_BITS + 1
+    side_spin = split_spin - 1
+    zero_tile = jnp.zeros((8, LANES), jnp.float32)
+    tiles = [(s, side) for s in range(BLOCK // SUB) for side in range(2)]
+
+    def device(core_index, chip):
+        return {"traj": first_traj + core_index, "amp": chip}
+
+    def remote(source, target, send, recv, where):
+        return pltpu.make_async_remote_copy(
+            src_ref=source,
+            dst_ref=target,
+            send_sem=send,
+            recv_sem=recv,
+            device_id=where,
+            device_id_type=pl.DeviceIdType.MESH,
+        )
+
+    other = device(1 - core, me)
+    barrier = pltpu.get_barrier_semaphore()
+    for flip_core in range(2):
+        for flip_chip in range(quarters):
+            if flip_core or flip_chip:
+                pl.semaphore_signal(
+                    barrier,
+                    inc=1,
+                    device_id=device(core ^ flip_core, me ^ flip_chip),
+                    device_id_type=pl.DeviceIdType.MESH,
+                )
+    own_channel[...] = jnp.full(own_channel.shape, channel_ref[0], jnp.int32)
+    pl.semaphore_wait(barrier, 2 * quarters - 1)
+
+    near_chip = me ^ (held ^ core)
+    far_chip = near_chip ^ 3
+
+    def piece(core_index, chip, slot):
+        source = block.at[pl.ds(pl.multiple_of(core_index * piece_rows, piece_rows), piece_rows)]
+        return remote(
+            source,
+            landing.at[me],
+            gather_send.at[slot],
+            gather_recv.at[me],
+            device(core_index, chip),
+        )
+
+    sends = [piece(core, far_chip, 0), piece(1 - core, far_chip, 1), piece(1 - core, near_chip, 2)]
+    for send in sends:
+        send.start()
+
+    @pl.when(jnp.logical_not(stays))
+    def _():
+        piece(core, near_chip, 3).start()
+
+    channel_copy = remote(
+        own_channel, other_channel, channel_sem.at[0], channel_sem.at[1], other
+    )
+    channel_copy.start()
+
+    crossed = lax.broadcasted_iota(jnp.int32, (BLOCK, BLOCK), 0)
+    crossed = crossed ^ lax.broadcasted_iota(jnp.int32, (BLOCK, BLOCK), 1)
+    for table, spins, axis in (
+        (row_table, [LANE_BITS + b for b in range(BLOCK_BITS)], 1),
+        (lane_table, [*range(LANE_BITS), side_spin], 0),
+    ):
+        value = jnp.zeros((BLOCK, BLOCK), jnp.float32)
+        for bit, spin in enumerate(spins):
+            value = jnp.where(crossed == 1 << bit, fields[spin], value)
+        hi, lo = split(value)
+        table[...] = jnp.concatenate([hi, hi, lo], axis=axis)
+
+    core_sign = (1 - 2 * core).astype(jnp.float32)
+    for side in range(2):
+        low_shape = (BLOCK, LANES)
+        low_pos = lax.broadcasted_iota(jnp.int32, low_shape, 0) * LANES
+        low_pos = low_pos + lax.broadcasted_iota(jnp.int32, low_shape, 1)
+        side_sign = 1.0 - 2.0 * side
+        low_real = jnp.zeros(low_shape, jnp.float32)
+        low_imag = jnp.zeros(low_shape, jnp.float32)
+        before = None
+        for spin in range(side_spin):
+            occupied = (lax.shift_right_logical(low_pos, spin) & 1).astype(jnp.float32)
+            sign = 1.0 - 2.0 * occupied
+            low_imag = low_imag - 0.5 * decays[spin] * occupied
+            if spin > 0:
+                low_real = low_real - couplings[spin - 1] * (before * sign)
+            before = sign
+        low_real = low_real - couplings[side_spin - 1] * side_sign * before
+        low_real = low_real - couplings[side_spin] * side_sign * core_sign
+        low_imag = low_imag - 0.5 * side * decays[side_spin]
+        low_imag = low_imag - 0.5 * core.astype(jnp.float32) * decays[split_spin]
+        diag_low[0, side] = low_real
+        diag_low[1, side] = low_imag
+
+    def high_diagonal(q):
+        signs = [core_sign]
+        real = jnp.float32(0.0)
+        imag = jnp.float32(0.0)
+        for b in range(SPINS - 1 - split_spin):
+            bit = (lax.shift_right_logical(q, b) & 1).astype(jnp.float32)
+            signs.append(1.0 - 2.0 * bit)
+            imag = imag - 0.5 * decays[split_spin + 1 + b] * bit
+            real = real - couplings[split_spin + b] * signs[b] * signs[b + 1]
+        return real, imag
+
+    def window(ref, lead, part, s, side):
+        return ref.at[(*lead, part, pl.ds(s * SUB, SUB), pl.ds(side * LANES, LANES))]
+
+    def total(values, slot):
+        count = len(values)
+        for k, value in enumerate(values):
+            own_sums[slot, 8 * k : 8 * k + 8] = value
+        copy = remote(
+            own_sums.at[slot, pl.ds(0, 8 * count)],
+            other_sums.at[slot, pl.ds(0, 8 * count)],
+            sums_send.at[slot],
+            sums_recv.at[slot],
+            other,
+        )
+        copy.start()
+        copy.wait()
+        return [
+            own_sums[slot, 8 * k : 8 * k + 8] + other_sums[slot, 8 * k : 8 * k + 8]
+            for k in range(count)
+        ]
+
+    def mate_copy(j, q):
+        return remote(basis.at[j, q], mate.at[q], mate_send.at[q], mate_recv.at[q], other)
+
+    @pl.when(stays)
+    def _():
+        def keep(i, carry):
+            rows = pl.multiple_of(i * SUB, SUB)
+            landing[me, pl.ds(rows, SUB), :] = block[
+                pl.ds(pl.multiple_of(core * piece_rows, piece_rows) + rows, SUB), :
+            ]
+            return carry
+
+        lax.fori_loop(0, piece_rows // SUB, keep, 0)
+
+    def arrival(chip):
+        return remote(
+            block.at[pl.ds(0, piece_rows)],
+            landing.at[chip],
+            gather_send.at[0],
+            gather_recv.at[chip],
+            other,
+        )
+
+    @pl.when(jnp.logical_not(stays))
+    def _():
+        arrival(me).wait_recv()
+
+    start_sq = zero_tile
+    for flip_chip in range(quarters):
+        q = me ^ flip_chip
+        if flip_chip:
+            arrival(q).wait_recv()
+
+        def start_norm(i, acc, q=q):
+            x = landing[q, pl.ds(pl.multiple_of(i * 128, 128), 128), :]
+            return acc + fold(x * x)
+
+        start_sq = lax.fori_loop(0, piece_rows // 128, start_norm, start_sq)
+    beta, inv_beta = scalar_sqrt(jnp.sum(total([start_sq], 1)[0]))
+
+    def start_vector(q, carry):
+        for s, side in tiles:
+            for part in range(2):
+                first = (side * BLOCK + s * SUB) * 2 + part
+                x = landing[q, pl.ds(first, SUB, stride=2), :]
+                window(basis, (0, q), part, s, side)[...] = x * inv_beta
+        mate_copy(0, q).start()
+        return carry
+
+    lax.fori_loop(0, quarters, start_vector, 0)
+
+    mat_rows = lax.broadcasted_iota(jnp.int32, (2 * KRYLOV, LANES), 0)
+    mat_cols = lax.broadcasted_iota(jnp.int32, (2 * KRYLOV, LANES), 1)
+    a_matrix = jnp.zeros((2 * KRYLOV, LANES), jnp.float32)
+
+    def put(matrix, k, j, real, imag):
+        a_real = time_step * imag
+        a_imag = -time_step * real
+        for r, c, value in (
+            (k, j, a_real),
+            (k, j + KRYLOV, -a_imag),
+            (k + KRYLOV, j, a_imag),
+            (k + KRYLOV, j + KRYLOV, a_real),
+        ):
+            matrix = jnp.where((mat_rows == r) & (mat_cols == c), value, matrix)
+        return matrix
+
+    high_fields = [fields[split_spin + 1 + b] for b in range(SPINS - 1 - split_spin)]
+    split_field = fields[split_spin]
+
+    for j in range(KRYLOV):
+        last = j + 1 == KRYLOV
+
+        def issue(q, flips, j=j):
+            for part in range(2):
+                hi, lo = split(basis[j, q, part])
+                flips[part] = dot(
+                    jnp.concatenate([row_table[...], hi, lo, hi], axis=1),
+                    jnp.concatenate([hi, lo, hi, lane_table[...]], axis=0),
+                )
+
+        def consume(q, flips, acc, j=j):
+            acc = list(acc)
+            real_high, imag_high = high_diagonal(q)
+            for s, side in tiles:
+                x = [window(basis, (j, q), part, s, side)[...] for part in range(2)]
+                f = [window(flips, (), part, s, side)[...] for part in range(2)]
+                for part in range(2):
+                    f[part] = f[part] + split_field * window(mate, (q,), part, s, side)[...]
+                    for b, field in enumerate(high_fields):
+                        f[part] = (
+                            f[part]
+                            + field * window(basis, (j, q ^ (1 << b)), part, s, side)[...]
+                        )
+                dr = window(diag_low, (0,), side, s, 0)[...] + real_high
+                di = window(diag_low, (1,), side, s, 0)[...] + imag_high
+                wr = dr * x[0] - di * x[1] - f[0]
+                wi = dr * x[1] + di * x[0] - f[1]
+                window(work, (q,), 0, s, side)[...] = wr
+                window(work, (q,), 1, s, side)[...] = wi
+                for k in range(j + 1):
+                    vr = window(basis, (k, q), 0, s, side)[...]
+                    vi = window(basis, (k, q), 1, s, side)[...]
+                    acc[2 * k] = acc[2 * k] + fold(vr * wr + vi * wi)
+                    acc[2 * k + 1] = acc[2 * k + 1] + fold(vr * wi - vi * wr)
+                acc[-1] = acc[-1] + fold(wr * wr + wi * wi)
+            return tuple(acc)
+
+        def apply_pair(i, acc, j=j):
+            even = 2 * i
+            odd = even + 1
+            mate_copy(j, even).wait()
+            mate_copy(j, odd).wait()
+            issue(odd, flips_odd)
+            acc = consume(even, flips_even, acc)
+            issue((even + 2) % quarters, flips_even)
+            return consume(odd, flips_odd, acc)
+
+        issue(0, flips_even)
+        sums = lax.fori_loop(0, quarters // 2, apply_pair, (zero_tile,) * (2 * j + 3))
+        coeffs = [jnp.sum(t) for t in total(sums, j % 2)]
+        for k in range(j + 1):
+            a_matrix = put(a_matrix, k, j, coeffs[2 * k], coeffs[2 * k + 1])
+        if last:
+            break
+        left = coeffs[-1]
+        for value in coeffs[:-1]:
+            left = left - value * value
+        norm, inv_norm = scalar_sqrt(left)
+        a_matrix = put(a_matrix, j + 1, j, norm, jnp.float32(0.0))
+
+        def subtract(q, carry, j=j, coeffs=coeffs, inv_norm=inv_norm):
+            for s, side in tiles:
+                rr = window(work, (q,), 0, s, side)[...]
+                ri = window(work, (q,), 1, s, side)[...]
+                for k in range(j + 1):
+                    vr = window(basis, (k, q), 0, s, side)[...]
+                    vi = window(basis, (k, q), 1, s, side)[...]
+                    hr, hm = coeffs[2 * k], coeffs[2 * k + 1]
+                    rr = rr - (hr * vr - hm * vi)
+                    ri = ri - (hr * vi + hm * vr)
+                window(basis, (j + 1, q), 0, s, side)[...] = rr * inv_norm
+                window(basis, (j + 1, q), 1, s, side)[...] = ri * inv_norm
+            mate_copy(j + 1, q).start()
+            return carry
+
+        lax.fori_loop(0, quarters, subtract, 0)
+
+    series = krylov_weights(a_matrix)
+    first = series[: 2 * KRYLOV, :] * beta
+    weights = [
+        jnp.sum(jnp.where((mat_rows == k) & (mat_cols == 0), first, 0.0))
+        for k in range(2 * KRYLOV)
+    ]
+    channel_copy.wait()
+    channel = jnp.where(stays, own_channel[...], other_channel[...])
+    sub_pos = lax.broadcasted_iota(jnp.int32, (SUB, LANES), 0) * LANES
+    sub_pos = sub_pos + lax.broadcasted_iota(jnp.int32, (SUB, LANES), 1)
+
+    def combine(q, acc):
+        high = (core << split_spin) + (q << (split_spin + 1))
+        for s, side in tiles:
+            pr = jnp.zeros((SUB, LANES), jnp.float32)
+            pi = jnp.zeros((SUB, LANES), jnp.float32)
+            for k in range(KRYLOV):
+                vr = window(basis, (k, q), 0, s, side)[...]
+                vi = window(basis, (k, q), 1, s, side)[...]
+                cr, ci = weights[k], weights[k + KRYLOV]
+                pr = pr + (cr * vr - ci * vi)
+                pi = pi + (cr * vi + ci * vr)
+            window(work, (q,), 0, s, side)[...] = pr
+            window(work, (q,), 1, s, side)[...] = pi
+            position = sub_pos + (high + (side << side_spin) + s * SUB * LANES)
+            occupied = lax.shift_right_logical(position, channel) & 1
+            acc = acc + fold(jnp.where(occupied == 1, pr * pr + pi * pi, 0.0))
+        return acc
+
+    jumped_sq = lax.fori_loop(0, quarters, combine, zero_tile)
+
+    def pack(target, q, part):
+        for s, side in tiles:
+            value = window(work, (q,), part, s, side)[...]
+            for b in range(SPINS - 1 - split_spin):
+                flipped = window(work, (q | (1 << b),), part, s, side)[...]
+                value = jnp.where(channel == split_spin + 1 + b, flipped, value)
+            target[s * SUB : (s + 1) * SUB, side * LANES : (side + 1) * LANES] = value
+
+    parcels = []
+    for part in range(2):
+        q = me ^ (1 << part)
+        pack(parcel.at[part], q, part)
+        copy = remote(
+            parcel.at[part],
+            pieces.at[core, part],
+            parcel_send.at[part],
+            parcel_recv.at[core, part],
+            device(held, q),
+        )
+        copy.start()
+        parcels.append(copy)
+    for part in range(2):
+        pack(parcel.at[2 + part], me, part)
+    home = remote(
+        parcel.at[pl.ds(2, 2)], pieces.at[core], parcel_send.at[2], parcel_recv.at[2, 0], other
+    )
+
+    @pl.when(jnp.logical_not(stays))
+    def _():
+        home.start()
+
+    @pl.when(stays)
+    def _():
+        for part in range(2):
+            pieces[core, part] = parcel[2 + part]
+
+    all_sq = jnp.sum(total([jumped_sq], 0)[0])
+    size = jnp.float32(quarters * 2 * piece_rows // 2 * LANES)
+    ratio = jnp.where(channel[:8] < SPINS, size / jnp.full((8, LANES), all_sq, jnp.float32), 1.0)
+    own_scale = jnp.sqrt(ratio)
+    own_sums[1, 0:8] = own_scale
+    scale_copy = remote(
+        own_sums.at[1, pl.ds(0, 8)], scale_out, scale_sem.at[0], scale_sem.at[1],
+        device(core, me ^ 1),
+    )
+
+    @pl.when(stays)
+    def _():
+        scale_copy.start()
+        scale_out[...] = own_scale
+        remote(
+            parcel.at[pl.ds(2, 2)], pieces.at[1 - core], parcel_send.at[2],
+            parcel_recv.at[2, 0], other,
+        ).wait_recv()
+        scale_copy.wait_send()
+
+    @pl.when(jnp.logical_not(stays))
+    def _():
+        for sender in range(2):
+            for part in range(2):
+                remote(
+                    parcel.at[part], pieces.at[sender, part], parcel_send.at[part],
+                    parcel_recv.at[sender, part], other,
+                ).wait_recv()
+        scale_copy.wait_recv()
+        home.wait_send()
+        piece(core, near_chip, 3).wait_send()
+
+    for copy in parcels:
+        copy.wait_send()
+    for send in sends:
+        send.wait_send()
+
+
+def lower_kernel(channel_ref, pieces, scale, out):
+    channel = channel_ref[0]
+    me = lax.axis_index("amp")
+    side_spin = LANE_BITS + BLOCK_BITS
+    in_lanes = channel < LANE_BITS
+    in_rows = jnp.logical_not(in_lanes) & (channel < side_spin)
+    lane_shift = jnp.where(in_lanes, lax.shift_left(1, channel), 0)
+    row_shift = jnp.where(in_rows, lax.shift_left(1, jnp.maximum(channel - LANE_BITS, 0)), 0)
+    near = jnp.where(row_shift < 8, row_shift, 0)
+    far = jnp.where(row_shift < 8, 0, row_shift)
+    lane_turn = (LANES - lane_shift) % LANES
+    row_turn = (8 - near) % 8
+    sub_pos = lax.broadcasted_iota(jnp.int32, (8, LANES), 0) * LANES
+    sub_pos = sub_pos + lax.broadcasted_iota(jnp.int32, (8, LANES), 1)
+    own = me * (4 * BLOCK * LANES)
+    factor = scale[...]
+
+    for half in range(2):
+        from_half = jnp.where(channel == side_spin + 1, 1, half)
+        for side in range(2):
+            from_side = jnp.where(channel == side_spin, 1, side)
+            columns = pl.ds(pl.multiple_of(from_side * LANES, LANES), LANES)
+
+            def lower(i, carry, half=half, side=side, from_half=from_half, columns=columns):
+                for t in range(8):
+                    local = i * 64 + t * 8
+                    base = (half * 2 + side) * BLOCK + local
+                    rows = pl.ds(pl.multiple_of(local | far, 8), 8)
+                    position = sub_pos + (own + base * LANES)
+                    vacant = (lax.shift_right_logical(position, channel) & 1) == 0
+                    for part in range(2):
+                        x = pieces[from_half, part, rows, columns]
+                        x = pltpu.roll(x, row_turn, 0)
+                        x = pltpu.roll(x, lane_turn, 1)
+                        x = jnp.where(vacant, x * factor, 0.0)
+                        out[pl.ds(base * 2 + part, 8, stride=2), :] = x
+                return carry
+
+            lax.fori_loop(0, BLOCK // 64, lower, 0)
+
+
+def paired_body(amplitudes, couplings, fields, decays, channel):
+    quarters = lax.axis_size("amp")
+    local_len = amplitudes.shape[2]
+    block_rows = local_len // LANES
+    vmem = pl.BlockSpec(memory_space=pltpu.VMEM)
+    smem = pl.BlockSpec(memory_space=pltpu.SMEM)
+    f32 = jnp.float32
+    dma = pltpu.SemaphoreType.DMA
+    sums_rows = 8 * (2 * KRYLOV + 1)
+    state = amplitudes.reshape(2, block_rows, LANES).transpose(1, 0, 2)
+    state = state.reshape(2 * block_rows, LANES)
+    pieces, scale = pl.pallas_call(
+        pair_kernel,
+        out_shape=(
+            jax.ShapeDtypeStruct((2, 2, BLOCK, BLOCK), f32),
+            jax.ShapeDtypeStruct((8, LANES), f32),
+        ),
+        in_specs=[smem] * 4 + [vmem],
+        out_specs=(vmem, vmem),
+        scratch_shapes=[
+            pltpu.VMEM((quarters, block_rows, LANES), f32),
+            pltpu.VMEM((KRYLOV, quarters, 2, BLOCK, BLOCK), f32),
+            pltpu.VMEM((quarters, 2, BLOCK, BLOCK), f32),
+            pltpu.VMEM((quarters, 2, BLOCK, BLOCK), f32),
+            pltpu.VMEM((2, BLOCK, BLOCK), f32),
+            pltpu.VMEM((2, BLOCK, BLOCK), f32),
+            pltpu.VMEM((BLOCK, 3 * BLOCK), jnp.bfloat16),
+            pltpu.VMEM((3 * BLOCK, BLOCK), jnp.bfloat16),
+            pltpu.VMEM((2, 2, BLOCK, LANES), f32),
+            pltpu.VMEM((2, sums_rows, LANES), f32),
+            pltpu.VMEM((2, sums_rows, LANES), f32),
+            pltpu.VMEM((SUB, LANES), jnp.int32),
+            pltpu.VMEM((SUB, LANES), jnp.int32),
+            pltpu.VMEM((4, BLOCK, BLOCK), f32),
+            dma((4,)),
+            dma((quarters,)),
+            dma((2,)),
+            dma((2,)),
+            dma((quarters,)),
+            dma((quarters,)),
+            dma((2,)),
+            dma((3,)),
+            dma((3, 2)),
+            dma((2,)),
+        ],
+        compiler_params=pltpu.CompilerParams(
+            collective_id=1, has_side_effects=True, vmem_limit_bytes=62 * 1024 * 1024
+        ),
+        name="pair",
+    )(channel, couplings, fields, decays, state)
+    lowered = pl.pallas_call(
+        lower_kernel,
+        out_shape=jax.ShapeDtypeStruct((2 * block_rows, LANES), f32),
+        in_specs=[smem, vmem, vmem],
+        out_specs=vmem,
+        name="lower",
+    )(channel, pieces, scale)
+    lowered = lowered.reshape(block_rows, 2, LANES).transpose(1, 0, 2)
+    return lowered.reshape(amplitudes.shape)
+
+
 def solution(mesh):
     placed = (P("traj", None, "amp"), P(), P(), P(), P("traj"))
-    return jax.shard_map(
-        body, mesh=mesh, in_specs=placed, out_specs=P("traj", None, "amp"), check_vma=False
-    )
+
+    def step(amplitudes, *rest):
+        trajectories = mesh.shape["traj"]
+        low_rows = amplitudes.shape[2] // mesh.shape["amp"] // LANES
+        paired = (
+            mesh.shape["amp"] == 4
+            and trajectories % 2 == 0
+            and amplitudes.shape[0] == trajectories
+            and low_rows == 4 * BLOCK
+        )
+        return jax.shard_map(
+            paired_body if paired else body,
+            mesh=mesh,
+            in_specs=placed,
+            out_specs=P("traj", None, "amp"),
+            check_vma=False,
+        )(amplitudes, *rest)
+
+    return step

time: 161 us -> 109 us (0.68)
  Pallas kernels: 154 us -> 108 us
  local copies, waits for them, and re-layouts: 5.12 us -> 0 us
    pallas_call x2, Pallas kernels: 154 us -> 108 us  [the longest x1 105 us: paired_body(): pl.pallas_call(pair_kernel, out_shape=(jax.ShapeDtypeStruct((2, 2, BLOCK,...]
    another operation x1 -> x0, local copies, waits for them, and re-layouts: 2.86 us -> none  [body(): return jnp.stack(results).reshape(amplitudes.shape)]
    unnamed x1 -> x0, local copies, waits for them, and re-layouts: 2.26 us -> none
where the time goes in v1:
time: 109 us
  Pallas kernels  108 us (99%)
    pallas_call x1, Pallas kernels, paired_body(): pl.pallas_call(pair_kernel, out_shape=(jax.ShapeDtypeStruct((2, 2, BLOCK,...  105 us
    pallas_call x1, Pallas kernels, paired_body(): pl.pallas_call(lower_kernel, out_shape=jax.ShapeDtypeStruct((2 * block_ro...  3.59 us

profile of v1, /device:TPU:1, one launch (start us, length us, event | category | flops | bytes accessed | tf_op | source)
XLA Modules:
  0.0 109.0 jit_solution(6576636456491550776)
XLA Ops:
  0.7 104.7 %pair.1 = (f32[2,2,256,256]{3,2,1,0:T(8,128)}, f32[8,128]{1,0:T(8,128)}) custom-call(s32[1]{0:T(128)S(6)} %copy.8.channel_ref, f32[18]{0:T(128)} %couplings.1, f32[19]{0:T(128)} %fields.1, f32[19]{0:T(128)} %decays.1, f32[2048,128]{1,0:T(8,128)} %bitcast.10), custom_call_target="tpu_custom_call" | custom-call | tf_op jit(solution)/shard_map/pair/pallas_call | solution.py:867
  105.4 3.6 %lower.1 = f32[2048,128]{1,0:T(8,128)} custom-call(s32[1]{0:T(128)S(6)} %copy.8.channel_ref, f32[2,2,256,256]{3,2,1,0:T(8,128)} %get-tuple-element.7.pieces, f32[8,128]{1,0:T(8,128)} %get-tuple-element.8.scale), custom_call_target="tpu_custom_call" | custom-call | tf_op jit(solution)/shard_map/lower/pallas_call | solution.py:906

commit v2 on v1

--- a/solution.py
+++ b/solution.py
@@ -1,3 +1,5 @@
+import math
+
 import jax
 import jax.numpy as jnp
 from jax import lax
@@ -402,25 +404,33 @@
     pieces,
     scale_out,
     landing,
+    mate_landing,
     basis,
+    mate,
     work,
-    mate,
+    mate_work,
     flips_even,
     flips_odd,
     row_table,
     lane_table,
-    diag_low,
+    diagonal,
     own_sums,
     other_sums,
+    own_rest,
+    other_rest,
+    scalars,
     own_channel,
     other_channel,
     parcel,
     gather_send,
     gather_recv,
+    forward_send,
+    forward_recv,
     sums_send,
     sums_recv,
-    mate_send,
-    mate_recv,
+    rest_sem,
+    work_send,
+    work_recv,
     channel_sem,
     parcel_send,
     parcel_recv,
@@ -492,6 +502,8 @@
     )
     channel_copy.start()
 
+    unit = fields[split_spin]
+    inv_unit = jnp.max(1.0 / jnp.full((8, LANES), unit, jnp.float32))
     crossed = lax.broadcasted_iota(jnp.int32, (BLOCK, BLOCK), 0)
     crossed = crossed ^ lax.broadcasted_iota(jnp.int32, (BLOCK, BLOCK), 1)
     for table, spins, axis in (
@@ -500,11 +512,14 @@
     ):
         value = jnp.zeros((BLOCK, BLOCK), jnp.float32)
         for bit, spin in enumerate(spins):
-            value = jnp.where(crossed == 1 << bit, fields[spin], value)
+            value = jnp.where(crossed == 1 << bit, fields[spin] * inv_unit, value)
         hi, lo = split(value)
         table[...] = jnp.concatenate([hi, hi, lo], axis=axis)
 
-    core_sign = (1 - 2 * core).astype(jnp.float32)
+    core_bit = core.astype(jnp.float32)
+    core_sign = 1.0 - 2.0 * core_bit
+    bond = [couplings[spin] * inv_unit for spin in range(SPINS - 1)]
+    loss = [0.5 * decays[spin] * inv_unit for spin in range(SPINS)]
     for side in range(2):
         low_shape = (BLOCK, LANES)
         low_pos = lax.broadcasted_iota(jnp.int32, low_shape, 0) * LANES
@@ -516,51 +531,54 @@
         for spin in range(side_spin):
             occupied = (lax.shift_right_logical(low_pos, spin) & 1).astype(jnp.float32)
             sign = 1.0 - 2.0 * occupied
-            low_imag = low_imag - 0.5 * decays[spin] * occupied
+            low_imag = low_imag - loss[spin] * occupied
             if spin > 0:
-                low_real = low_real - couplings[spin - 1] * (before * sign)
+                low_real = low_real - bond[spin - 1] * (before * sign)
             before = sign
-        low_real = low_real - couplings[side_spin - 1] * side_sign * before
-        low_real = low_real - couplings[side_spin] * side_sign * core_sign
-        low_imag = low_imag - 0.5 * side * decays[side_spin]
-        low_imag = low_imag - 0.5 * core.astype(jnp.float32) * decays[split_spin]
-        diag_low[0, side] = low_real
-        diag_low[1, side] = low_imag
-
-    def high_diagonal(q):
-        signs = [core_sign]
-        real = jnp.float32(0.0)
-        imag = jnp.float32(0.0)
-        for b in range(SPINS - 1 - split_spin):
-            bit = (lax.shift_right_logical(q, b) & 1).astype(jnp.float32)
-            signs.append(1.0 - 2.0 * bit)
-            imag = imag - 0.5 * decays[split_spin + 1 + b] * bit
-            real = real - couplings[split_spin + b] * signs[b] * signs[b + 1]
-        return real, imag
+        low_real = low_real - bond[side_spin - 1] * side_sign * before
+        low_real = low_real - bond[side_spin] * side_sign * core_sign
+        low_imag = low_imag - side * loss[side_spin] - core_bit * loss[split_spin]
+        for q in range(quarters):
+            bits = [(q >> b) & 1 for b in range(SPINS - 1 - split_spin)]
+            signs = [core_sign] + [1.0 - 2.0 * bit for bit in bits]
+            real, imag = low_real, low_imag
+            for b, bit in enumerate(bits):
+                real = real - bond[split_spin + b] * (signs[b] * signs[b + 1])
+                imag = imag - bit * loss[split_spin + 1 + b]
+            diagonal[q, 0, side] = real
+            diagonal[q, 1, side] = imag
 
     def window(ref, lead, part, s, side):
         return ref.at[(*lead, part, pl.ds(s * SUB, SUB), pl.ds(side * LANES, LANES))]
 
-    def total(values, slot):
-        count = len(values)
-        for k, value in enumerate(values):
-            own_sums[slot, 8 * k : 8 * k + 8] = value
-        copy = remote(
+    def sums_copy(count, slot):
+        return remote(
             own_sums.at[slot, pl.ds(0, 8 * count)],
             other_sums.at[slot, pl.ds(0, 8 * count)],
             sums_send.at[slot],
             sums_recv.at[slot],
             other,
         )
-        copy.start()
-        copy.wait()
-        return [
-            own_sums[slot, 8 * k : 8 * k + 8] + other_sums[slot, 8 * k : 8 * k + 8]
-            for k in range(count)
-        ]
-
-    def mate_copy(j, q):
-        return remote(basis.at[j, q], mate.at[q], mate_send.at[q], mate_recv.at[q], other)
+
+    def start_sums(values, slot):
+        for k, value in enumerate(values):
+            own_sums[slot, 8 * k : 8 * k + 8] = value
+        sums_copy(len(values), slot).start()
+
+    def finish_sums(count, slot):
+        sums_copy(count, slot).wait()
+        both = [ref[slot, : 8 * count] for ref in (own_sums, other_sums)]
+        both = both[0] + both[1]
+        return [jnp.sum(both[8 * k : 8 * k + 8]) for k in range(count)]
+
+    def work_copy(slot, q):
+        return remote(
+            work.at[slot, q],
+            mate_work.at[slot, q],
+            work_send.at[slot, q],
+            work_recv.at[slot, q],
+            other,
+        )
 
     @pl.when(stays)
     def _():
@@ -582,136 +600,268 @@
             other,
         )
 
+    def forward(chip):
+        return remote(
+            landing.at[chip],
+            mate_landing.at[chip],
+            forward_send.at[chip],
+            forward_recv.at[chip],
+            other,
+        )
+
     @pl.when(jnp.logical_not(stays))
     def _():
         arrival(me).wait_recv()
 
-    start_sq = zero_tile
+    def square(ref, q, acc):
+        def add(i, acc):
+            x = ref[q, pl.ds(pl.multiple_of(i * 128, 128), 128), :]
+            return acc + fold(x * x)
+
+        return lax.fori_loop(0, piece_rows // 128, add, acc)
+
+    own_sq = zero_tile
     for flip_chip in range(quarters):
         q = me ^ flip_chip
         if flip_chip:
             arrival(q).wait_recv()
-
-        def start_norm(i, acc, q=q):
-            x = landing[q, pl.ds(pl.multiple_of(i * 128, 128), 128), :]
-            return acc + fold(x * x)
-
-        start_sq = lax.fori_loop(0, piece_rows // 128, start_norm, start_sq)
-    beta, inv_beta = scalar_sqrt(jnp.sum(total([start_sq], 1)[0]))
+        forward(q).start()
+        own_sq = square(landing, q, own_sq)
+    mate_sq = zero_tile
+    for flip_chip in range(quarters):
+        q = me ^ flip_chip
+        forward(q).wait()
+        mate_sq = square(mate_landing, q, mate_sq)
+    beta, inv_beta = scalar_sqrt(jnp.sum(own_sq + mate_sq))
 
     def start_vector(q, carry):
+        for source, target in ((landing, basis), (mate_landing, mate)):
+            for s, side in tiles:
+                for part in range(2):
+                    first = (side * BLOCK + s * SUB) * 2 + part
+                    x = source[q, pl.ds(first, SUB, stride=2), :]
+                    window(target, (0, q), part, s, side)[...] = x * inv_beta
+        return carry
+
+    lax.fori_loop(0, quarters, start_vector, 0)
+
+    high_fields = [fields[split_spin + 1 + b] * inv_unit for b in range(SPINS - 1 - split_spin)]
+    flips = (flips_even, flips_odd)
+
+    def issue(j, q):
+        for part in range(2):
+            hi, lo = split(basis[j, q, part])
+            flips[q % 2][part] = dot(
+                jnp.concatenate([row_table[...], hi, lo, hi], axis=1),
+                jnp.concatenate([hi, lo, hi, lane_table[...]], axis=0),
+            )
+
+    def inner(k, q, s, side, wr, wi):
+        vr = window(basis, (k, q), 0, s, side)[...]
+        vi = window(basis, (k, q), 1, s, side)[...]
+        return fold(vr * wr + vi * wi), fold(vr * wi - vi * wr)
+
+    def consume(j, q, acc, against, keep):
+        slot = j % 2
         for s, side in tiles:
+            x = [window(basis, (j, q), part, s, side)[...] for part in range(2)]
+            f = []
             for part in range(2):
-                first = (side * BLOCK + s * SUB) * 2 + part
-                x = landing[q, pl.ds(first, SUB, stride=2), :]
-                window(basis, (0, q), part, s, side)[...] = x * inv_beta
-        mate_copy(0, q).start()
-        return carry
-
-    lax.fori_loop(0, quarters, start_vector, 0)
-
-    mat_rows = lax.broadcasted_iota(jnp.int32, (2 * KRYLOV, LANES), 0)
-    mat_cols = lax.broadcasted_iota(jnp.int32, (2 * KRYLOV, LANES), 1)
-    a_matrix = jnp.zeros((2 * KRYLOV, LANES), jnp.float32)
-
-    def put(matrix, k, j, real, imag):
-        a_real = time_step * imag
-        a_imag = -time_step * real
-        for r, c, value in (
-            (k, j, a_real),
-            (k, j + KRYLOV, -a_imag),
-            (k + KRYLOV, j, a_imag),
-            (k + KRYLOV, j + KRYLOV, a_real),
-        ):
-            matrix = jnp.where((mat_rows == r) & (mat_cols == c), value, matrix)
-        return matrix
-
-    high_fields = [fields[split_spin + 1 + b] for b in range(SPINS - 1 - split_spin)]
-    split_field = fields[split_spin]
-
-    for j in range(KRYLOV):
-        last = j + 1 == KRYLOV
-
-        def issue(q, flips, j=j):
-            for part in range(2):
-                hi, lo = split(basis[j, q, part])
-                flips[part] = dot(
-                    jnp.concatenate([row_table[...], hi, lo, hi], axis=1),
-                    jnp.concatenate([hi, lo, hi, lane_table[...]], axis=0),
-                )
-
-        def consume(q, flips, acc, j=j):
-            acc = list(acc)
-            real_high, imag_high = high_diagonal(q)
-            for s, side in tiles:
-                x = [window(basis, (j, q), part, s, side)[...] for part in range(2)]
-                f = [window(flips, (), part, s, side)[...] for part in range(2)]
-                for part in range(2):
-                    f[part] = f[part] + split_field * window(mate, (q,), part, s, side)[...]
-                    for b, field in enumerate(high_fields):
-                        f[part] = (
-                            f[part]
-                            + field * window(basis, (j, q ^ (1 << b)), part, s, side)[...]
-                        )
-                dr = window(diag_low, (0,), side, s, 0)[...] + real_high
-                di = window(diag_low, (1,), side, s, 0)[...] + imag_high
-                wr = dr * x[0] - di * x[1] - f[0]
-                wi = dr * x[1] + di * x[0] - f[1]
-                window(work, (q,), 0, s, side)[...] = wr
-                window(work, (q,), 1, s, side)[...] = wi
-                for k in range(j + 1):
-                    vr = window(basis, (k, q), 0, s, side)[...]
-                    vi = window(basis, (k, q), 1, s, side)[...]
-                    acc[2 * k] = acc[2 * k] + fold(vr * wr + vi * wi)
-                    acc[2 * k + 1] = acc[2 * k + 1] + fold(vr * wi - vi * wr)
+                value = window(flips[q % 2], (), part, s, side)[...]
+                value = value + window(mate, (slot, q), part, s, side)[...]
+                for b, field in enumerate(high_fields):
+                    value = value + field * window(basis, (j, q ^ (1 << b)), part, s, side)[...]
+                f.append(value)
+            dr = window(diagonal, (q, 0), side, s, 0)[...]
+            di = window(diagonal, (q, 1), side, s, 0)[...]
+            wr = dr * x[0] - di * x[1] - f[0]
+            wi = dr * x[1] + di * x[0] - f[1]
+            for n, k in enumerate(against):
+                real, imag = inner(k, q, s, side, wr, wi)
+                acc[2 * n] = acc[2 * n] + real
+                acc[2 * n + 1] = acc[2 * n + 1] + imag
+            if keep:
+                window(work, (slot, q), 0, s, side)[...] = wr
+                window(work, (slot, q), 1, s, side)[...] = wi
                 acc[-1] = acc[-1] + fold(wr * wr + wi * wi)
-            return tuple(acc)
-
-        def apply_pair(i, acc, j=j):
-            even = 2 * i
-            odd = even + 1
-            mate_copy(j, even).wait()
-            mate_copy(j, odd).wait()
-            issue(odd, flips_odd)
-            acc = consume(even, flips_even, acc)
-            issue((even + 2) % quarters, flips_even)
-            return consume(odd, flips_odd, acc)
-
-        issue(0, flips_even)
-        sums = lax.fori_loop(0, quarters // 2, apply_pair, (zero_tile,) * (2 * j + 3))
-        coeffs = [jnp.sum(t) for t in total(sums, j % 2)]
-        for k in range(j + 1):
-            a_matrix = put(a_matrix, k, j, coeffs[2 * k], coeffs[2 * k + 1])
-        if last:
-            break
+
+    def apply(j, against, keep):
+        acc = [zero_tile] * (2 * len(against) + keep)
+        for q in range(quarters):
+            if q + 1 < quarters:
+                issue(j, q + 1)
+            consume(j, q, acc, against, keep)
+            if keep:
+                work_copy(j % 2, q).start()
+        return acc
+
+    def rest_inner(j):
+        slot = j % 2
+
+        def one(k, carry):
+            def add(q, acc):
+                real, imag = acc
+                for s, side in tiles:
+                    wr = window(work, (slot, q), 0, s, side)[...]
+                    wi = window(work, (slot, q), 1, s, side)[...]
+                    more = inner(k, q, s, side, wr, wi)
+                    real, imag = real + more[0], imag + more[1]
+                return real, imag
+
+            real, imag = lax.fori_loop(0, quarters, add, (zero_tile, zero_tile))
+            own_rest[j, k, 0] = real
+            own_rest[j, k, 1] = imag
+            return carry
+
+        lax.fori_loop(0, j - 1, one, 0)
+
+    def step(j, first):
+        slot = j % 2
+        against = [j] if first else [j, j - 1]
+        count = 2 * len(against) + 1
+        start_sums(apply(j, against, True), slot)
+        if not first:
+            rest_inner(j)
+        coeffs = finish_sums(count, slot)
         left = coeffs[-1]
         for value in coeffs[:-1]:
             left = left - value * value
         norm, inv_norm = scalar_sqrt(left)
-        a_matrix = put(a_matrix, j + 1, j, norm, jnp.float32(0.0))
-
-        def subtract(q, carry, j=j, coeffs=coeffs, inv_norm=inv_norm):
+        for n, value in enumerate(coeffs[:-1]):
+            scalars[j, n] = value
+        scalars[j, 4] = norm
+        scalars[j, 5] = inv_norm
+
+        def subtract(q, w_ref, u_ref, now, before, after):
             for s, side in tiles:
-                rr = window(work, (q,), 0, s, side)[...]
-                ri = window(work, (q,), 1, s, side)[...]
-                for k in range(j + 1):
-                    vr = window(basis, (k, q), 0, s, side)[...]
-                    vi = window(basis, (k, q), 1, s, side)[...]
-                    hr, hm = coeffs[2 * k], coeffs[2 * k + 1]
+                rr = window(w_ref, (slot, q), 0, s, side)[...]
+                ri = window(w_ref, (slot, q), 1, s, side)[...]
+                for n, lead in enumerate([now] if first else [now, before]):
+                    vr = window(u_ref, (lead, q), 0, s, side)[...]
+                    vi = window(u_ref, (lead, q), 1, s, side)[...]
+                    hr, hm = coeffs[2 * n], coeffs[2 * n + 1]
                     rr = rr - (hr * vr - hm * vi)
                     ri = ri - (hr * vi + hm * vr)
-                window(basis, (j + 1, q), 0, s, side)[...] = rr * inv_norm
-                window(basis, (j + 1, q), 1, s, side)[...] = ri * inv_norm
-            mate_copy(j + 1, q).start()
-            return carry
-
-        lax.fori_loop(0, quarters, subtract, 0)
-
-    series = krylov_weights(a_matrix)
-    first = series[: 2 * KRYLOV, :] * beta
+                window(u_ref, (after, q), 0, s, side)[...] = rr * inv_norm
+                window(u_ref, (after, q), 1, s, side)[...] = ri * inv_norm
+
+        subtract(0, work, basis, j, j - 1, j + 1)
+        issue(j + 1, 0)
+        for q in range(1, quarters):
+            subtract(q, work, basis, j, j - 1, j + 1)
+        for q in range(quarters):
+            work_copy(slot, q).wait()
+        for q in range(quarters):
+            subtract(q, mate_work, mate, slot, 1 - slot, 1 - slot)
+
+    final = KRYLOV - 1
+    issue(0, 0)
+    step(0, True)
+
+    def later(j, carry):
+        step(j, False)
+        return carry
+
+    lax.fori_loop(1, final, later, 0)
+    rest_copy = remote(own_rest, other_rest, rest_sem.at[0], rest_sem.at[1], other)
+    rest_copy.start()
+    start_sums(apply(final, list(range(KRYLOV)), False), final % 2)
+    rest_copy.wait()
+    sub = lax.broadcasted_iota(jnp.int32, (8, LANES), 0)
+    lane = lax.broadcasted_iota(jnp.int32, (8, LANES), 1)
+
+    def put(tile, where, value):
+        return jnp.where(where, value, tile)
+
+    gram = [jnp.where(sub == lane, 1.0, 0.0).astype(jnp.float32), zero_tile]
+    projected = [zero_tile, zero_tile]
+    column = {j: [zero_tile, zero_tile] for j in range(3)}
+    across = {j: [zero_tile, zero_tile] for j in range(3)}
+    for j in range(final):
+        here = lane == j
+        alpha = [scalars[j, 0], scalars[j, 1]]
+        bravo = [scalars[j, 2], scalars[j, 3]]
+        for part in range(2):
+            projected[part] = put(projected[part], here & (sub == j), alpha[part])
+            if j > 0:
+                projected[part] = put(projected[part], here & (sub == j - 1), bravo[part])
+        projected[0] = put(projected[0], here & (sub == j + 1), scalars[j, 4])
+        if j < 2:
+            continue
+        down = [zero_tile, zero_tile]
+        along = [zero_tile, zero_tile]
+        for k in range(j - 1):
+            for part in range(2):
+                value = jnp.sum(own_rest[j, k, part] + other_rest[j, k, part])
+                down[part] = put(down[part], sub == k, value)
+                along[part] = put(along[part], lane == k, value)
+        for made, new in ((column, down), (across, along)):
+            for value, old in ((alpha, made[j]), (bravo, made[j - 1])):
+                new[0] = new[0] - (value[0] * old[0] - value[1] * old[1])
+                new[1] = new[1] - (value[0] * old[1] + value[1] * old[0])
+            made[j + 1] = [part * scalars[j, 5] for part in new]
+        gram[0] = gram[0] + jnp.where(lane == j + 1, column[j + 1][0], 0.0)
+        gram[0] = gram[0] + jnp.where(sub == j + 1, across[j + 1][0], 0.0)
+        gram[1] = gram[1] + jnp.where(lane == j + 1, column[j + 1][1], 0.0)
+        gram[1] = gram[1] - jnp.where(sub == j + 1, across[j + 1][1], 0.0)
+
+    targets = finish_sums(2 * KRYLOV, final % 2)
+    for k in range(KRYLOV):
+        for part in range(2):
+            gram[part] = put(gram[part], (lane == KRYLOV) & (sub == k), targets[2 * k + part])
+
+    def column_of(tile, k):
+        return jnp.broadcast_to(tile[:, k : k + 1], tile.shape)
+
+    def row_of(tile, k):
+        return jnp.broadcast_to(tile[k : k + 1, :], tile.shape)
+
+    for p in range(KRYLOV):
+        row = [row_of(tile, p) for tile in gram]
+        factor = [column_of(tile, p) for tile in gram]
+        inverse = 1.0 / row_of(factor[0], p)
+        row = [tile * inverse for tile in row]
+        less = (
+            factor[0] * row[0] - factor[1] * row[1],
+            factor[0] * row[1] + factor[1] * row[0],
+        )
+        gram = [jnp.where(sub == p, row[n], gram[n] - less[n]) for n in range(2)]
+    for part in range(2):
+        projected[part] = put(projected[part], lane == final, column_of(gram[part], KRYLOV))
+
+    def product(a, b):
+        real, imag = zero_tile, zero_tile
+        for k in range(KRYLOV):
+            ar, ai = column_of(a[0], k), column_of(a[1], k)
+            br, bi = row_of(b[0], k), row_of(b[1], k)
+            real = real + (ar * br - ai * bi)
+            imag = imag + (ar * bi + ai * br)
+        return real, imag
+
+    inside = lane < KRYLOV
+    pace = unit * (time_step / 2.0**squarings)
+    first = (
+        jnp.where(inside, projected[1] * pace, 0.0),
+        jnp.where(inside, projected[0] * -pace, 0.0),
+    )
+    second = product(first, first)
+    third = product(second, first)
+    identity = jnp.where(sub == lane, 1.0, 0.0).astype(jnp.float32)
+    series = None
+    for low in range(taylor_order // 3 * 3, -1, -3):
+        terms = [identity * (1.0 / math.factorial(low)), zero_tile]
+        for n, power in ((low + 1, first), (low + 2, second)):
+            if n <= taylor_order:
+                terms = [t + p * (1.0 / math.factorial(n)) for t, p in zip(terms, power)]
+        if series is not None:
+            terms = [t + p for t, p in zip(terms, product(third, series))]
+        series = terms
+    for repeat in range(squarings):
+        series = product(series, series)
     weights = [
-        jnp.sum(jnp.where((mat_rows == k) & (mat_cols == 0), first, 0.0))
-        for k in range(2 * KRYLOV)
+        jnp.sum(jnp.where((sub == k) & (lane == 0), tile * beta, 0.0))
+        for tile in series
+        for k in range(KRYLOV)
     ]
     channel_copy.wait()
     channel = jnp.where(stays, own_channel[...], other_channel[...])
@@ -729,8 +879,8 @@
                 cr, ci = weights[k], weights[k + KRYLOV]
                 pr = pr + (cr * vr - ci * vi)
                 pi = pi + (cr * vi + ci * vr)
-            window(work, (q,), 0, s, side)[...] = pr
-            window(work, (q,), 1, s, side)[...] = pi
+            window(work, (0, q), 0, s, side)[...] = pr
+            window(work, (0, q), 1, s, side)[...] = pi
             position = sub_pos + (high + (side << side_spin) + s * SUB * LANES)
             occupied = lax.shift_right_logical(position, channel) & 1
             acc = acc + fold(jnp.where(occupied == 1, pr * pr + pi * pi, 0.0))
@@ -738,11 +888,13 @@
 
     jumped_sq = lax.fori_loop(0, quarters, combine, zero_tile)
 
+    start_sums([jumped_sq], 0)
+
     def pack(target, q, part):
         for s, side in tiles:
-            value = window(work, (q,), part, s, side)[...]
+            value = window(work, (0, q), part, s, side)[...]
             for b in range(SPINS - 1 - split_spin):
-                flipped = window(work, (q | (1 << b),), part, s, side)[...]
+                flipped = window(work, (0, q | (1 << b)), part, s, side)[...]
                 value = jnp.where(channel == split_spin + 1 + b, flipped, value)
             target[s * SUB : (s + 1) * SUB, side * LANES : (side + 1) * LANES] = value
 
@@ -774,7 +926,7 @@
         for part in range(2):
             pieces[core, part] = parcel[2 + part]
 
-    all_sq = jnp.sum(total([jumped_sq], 0)[0])
+    all_sq = finish_sums(1, 0)[0]
     size = jnp.float32(quarters * 2 * piece_rows // 2 * LANES)
     ratio = jnp.where(channel[:8] < SPINS, size / jnp.full((8, LANES), all_sq, jnp.float32), 1.0)
     own_scale = jnp.sqrt(ratio)
@@ -874,25 +1026,33 @@
         out_specs=(vmem, vmem),
         scratch_shapes=[
             pltpu.VMEM((quarters, block_rows, LANES), f32),
+            pltpu.VMEM((quarters, block_rows, LANES), f32),
             pltpu.VMEM((KRYLOV, quarters, 2, BLOCK, BLOCK), f32),
-            pltpu.VMEM((quarters, 2, BLOCK, BLOCK), f32),
-            pltpu.VMEM((quarters, 2, BLOCK, BLOCK), f32),
+            pltpu.VMEM((2, quarters, 2, BLOCK, BLOCK), f32),
+            pltpu.VMEM((2, quarters, 2, BLOCK, BLOCK), f32),
+            pltpu.VMEM((2, quarters, 2, BLOCK, BLOCK), f32),
             pltpu.VMEM((2, BLOCK, BLOCK), f32),
             pltpu.VMEM((2, BLOCK, BLOCK), f32),
             pltpu.VMEM((BLOCK, 3 * BLOCK), jnp.bfloat16),
             pltpu.VMEM((3 * BLOCK, BLOCK), jnp.bfloat16),
-            pltpu.VMEM((2, 2, BLOCK, LANES), f32),
+            pltpu.VMEM((quarters, 2, 2, BLOCK, LANES), f32),
             pltpu.VMEM((2, sums_rows, LANES), f32),
             pltpu.VMEM((2, sums_rows, LANES), f32),
+            pltpu.VMEM((KRYLOV - 1, KRYLOV - 3, 2, 8, LANES), f32),
+            pltpu.VMEM((KRYLOV - 1, KRYLOV - 3, 2, 8, LANES), f32),
+            pltpu.SMEM((KRYLOV - 1, 6), f32),
             pltpu.VMEM((SUB, LANES), jnp.int32),
             pltpu.VMEM((SUB, LANES), jnp.int32),
             pltpu.VMEM((4, BLOCK, BLOCK), f32),
             dma((4,)),
             dma((quarters,)),
+            dma((quarters,)),
+            dma((quarters,)),
             dma((2,)),
             dma((2,)),
-            dma((quarters,)),
-            dma((quarters,)),
+            dma((2,)),
+            dma((2, quarters)),
+            dma((2, quarters)),
             dma((2,)),
             dma((3,)),
             dma((3, 2)),

time: 109 us -> 106 us (0.972)
  Pallas kernels: 108 us -> 105 us
    pallas_call x1, Pallas kernels: 105 us -> 102 us  [paired_body(): pl.pallas_call(pair_kernel, out_shape=(jax.ShapeDtypeStruct((2, 2, BLOCK,...]
where the time goes in v2:
time: 106 us
  Pallas kernels  105 us (99%)
    pallas_call x1, Pallas kernels, paired_body(): pl.pallas_call(pair_kernel, out_shape=(jax.ShapeDtypeStruct((2, 2, BLOCK,...  102 us
    pallas_call x1, Pallas kernels, paired_body(): pl.pallas_call(lower_kernel, out_shape=jax.ShapeDtypeStruct((2 * block_ro...  3.59 us

profile of v2, /device:TPU:1, one launch (start us, length us, event | category | flops | bytes accessed | tf_op | source)
XLA Modules:
  0.0 106.0 jit_solution(689010347353692883)
XLA Ops:
  0.7 101.8 %pair.1 = (f32[2,2,256,256]{3,2,1,0:T(8,128)}, f32[8,128]{1,0:T(8,128)}) custom-call(s32[1]{0:T(128)S(6)} %copy.8.channel_ref, f32[18]{0:T(128)} %couplings.1, f32[19]{0:T(128)} %fields.1, f32[19]{0:T(128)} %decays.1, f32[2048,128]{1,0:T(8,128)} %bitcast.10), custom_call_target="tpu_custom_call" | custom-call | tf_op jit(solution)/shard_map/pair/pallas_call | solution.py:1019
  102.4 3.6 %lower.1 = f32[2048,128]{1,0:T(8,128)} custom-call(s32[1]{0:T(128)S(6)} %copy.8.channel_ref, f32[2,2,256,256]{3,2,1,0:T(8,128)} %get-tuple-element.7.pieces, f32[8,128]{1,0:T(8,128)} %get-tuple-element.8.scale), custom_call_target="tpu_custom_call" | custom-call | tf_op jit(solution)/shard_map/lower/pallas_call | solution.py:1066

commit v3 on v2

--- a/solution.py
+++ b/solution.py
@@ -393,6 +393,7 @@
 
 BLOCK = 256
 BLOCK_BITS = 8
+TILE = 16
 
 
 def pair_kernel(
@@ -409,8 +410,8 @@
     mate,
     work,
     mate_work,
-    flips_even,
-    flips_odd,
+    flips,
+    splits,
     row_table,
     lane_table,
     diagonal,
@@ -447,7 +448,8 @@
     split_spin = LANE_BITS + BLOCK_BITS + 1
     side_spin = split_spin - 1
     zero_tile = jnp.zeros((8, LANES), jnp.float32)
-    tiles = [(s, side) for s in range(BLOCK // SUB) for side in range(2)]
+    tiles = [(s, side) for s in range(BLOCK // TILE) for side in range(2)]
+    half = BLOCK // 2
 
     def device(core_index, chip):
         return {"traj": first_traj + core_index, "amp": chip}
@@ -549,7 +551,7 @@
             diagonal[q, 1, side] = imag
 
     def window(ref, lead, part, s, side):
-        return ref.at[(*lead, part, pl.ds(s * SUB, SUB), pl.ds(side * LANES, LANES))]
+        return ref.at[(*lead, part, pl.ds(s * TILE, TILE), pl.ds(side * LANES, LANES))]
 
     def sums_copy(count, slot):
         return remote(
@@ -571,12 +573,13 @@
         both = both[0] + both[1]
         return [jnp.sum(both[8 * k : 8 * k + 8]) for k in range(count)]
 
-    def work_copy(slot, q):
+    def work_copy(slot, n):
+        pair = (pl.ds(2 * (n // 2), 2), slice(None), pl.ds(n % 2 * half, half))
         return remote(
-            work.at[slot, q],
-            mate_work.at[slot, q],
-            work_send.at[slot, q],
-            work_recv.at[slot, q],
+            work.at[(slot, *pair)],
+            mate_work.at[(slot, *pair)],
+            work_send.at[slot, n],
+            work_recv.at[slot, n],
             other,
         )
 
@@ -590,6 +593,8 @@
             return carry
 
         lax.fori_loop(0, piece_rows // SUB, keep, 0)
+
+    mate[1, pl.ds(2, 2)] = jnp.zeros((2, 2, BLOCK, BLOCK), jnp.float32)
 
     def arrival(chip):
         return remote(
@@ -634,77 +639,111 @@
         mate_sq = square(mate_landing, q, mate_sq)
     beta, inv_beta = scalar_sqrt(jnp.sum(own_sq + mate_sq))
 
+    def put_split(q, part, s, side, x):
+        for n, term in enumerate(split(x)):
+            window(splits, (q, part), n, s, side)[...] = term
+
     def start_vector(q, carry):
-        for source, target in ((landing, basis), (mate_landing, mate)):
-            for s, side in tiles:
-                for part in range(2):
-                    first = (side * BLOCK + s * SUB) * 2 + part
-                    x = source[q, pl.ds(first, SUB, stride=2), :]
-                    window(target, (0, q), part, s, side)[...] = x * inv_beta
+        for s, side in tiles:
+            for part in range(2):
+                rows = pl.ds((side * BLOCK + s * TILE) * 2 + part, TILE, stride=2)
+                x = landing[q, rows, :] * inv_beta
+                window(basis, (0, q), part, s, side)[...] = x
+                put_split(q, part, s, side, x)
+                window(mate, (0, q), part, s, side)[...] = mate_landing[q, rows, :] * inv_beta
         return carry
 
     lax.fori_loop(0, quarters, start_vector, 0)
 
     high_fields = [fields[split_spin + 1 + b] * inv_unit for b in range(SPINS - 1 - split_spin)]
-    flips = (flips_even, flips_odd)
-
-    def issue(j, q):
+
+    def issue(q):
         for part in range(2):
-            hi, lo = split(basis[j, q, part])
-            flips[q % 2][part] = dot(
+            hi, lo = splits[q, part, 0], splits[q, part, 1]
+            flips[q, part] = dot(
                 jnp.concatenate([row_table[...], hi, lo, hi], axis=1),
                 jnp.concatenate([hi, lo, hi, lane_table[...]], axis=0),
             )
 
-    def inner(k, q, s, side, wr, wi):
-        vr = window(basis, (k, q), 0, s, side)[...]
-        vi = window(basis, (k, q), 1, s, side)[...]
-        return fold(vr * wr + vi * wi), fold(vr * wi - vi * wr)
-
-    def consume(j, q, acc, against, keep):
+    def pairing(v, w):
+        return fold(v[0] * w[0] + v[1] * w[1]), fold(v[0] * w[1] - v[1] * w[0])
+
+    def load(ref, lead, s, side):
+        return [window(ref, lead, part, s, side)[...] for part in range(2)]
+
+    def consume(j, pair, acc, before, norm, send):
         slot = j % 2
         for s, side in tiles:
-            x = [window(basis, (j, q), part, s, side)[...] for part in range(2)]
-            f = []
-            for part in range(2):
-                value = window(flips[q % 2], (), part, s, side)[...]
-                value = value + window(mate, (slot, q), part, s, side)[...]
-                for b, field in enumerate(high_fields):
-                    value = value + field * window(basis, (j, q ^ (1 << b)), part, s, side)[...]
-                f.append(value)
-            dr = window(diagonal, (q, 0), side, s, 0)[...]
-            di = window(diagonal, (q, 1), side, s, 0)[...]
-            wr = dr * x[0] - di * x[1] - f[0]
-            wi = dr * x[1] + di * x[0] - f[1]
-            for n, k in enumerate(against):
-                real, imag = inner(k, q, s, side, wr, wi)
-                acc[2 * n] = acc[2 * n] + real
-                acc[2 * n + 1] = acc[2 * n + 1] + imag
-            if keep:
-                window(work, (slot, q), 0, s, side)[...] = wr
-                window(work, (slot, q), 1, s, side)[...] = wi
-                acc[-1] = acc[-1] + fold(wr * wr + wi * wi)
-
-    def apply(j, against, keep):
-        acc = [zero_tile] * (2 * len(against) + keep)
-        for q in range(quarters):
-            if q + 1 < quarters:
-                issue(j, q + 1)
-            consume(j, q, acc, against, keep)
-            if keep:
-                work_copy(j % 2, q).start()
+            chosen = (2 * pair, 2 * pair + 1)
+            x = [load(basis, (j, q), s, side) for q in chosen]
+            for n, q in enumerate(chosen):
+                made = load(flips, (q,), s, side)
+                near = load(mate, (slot, q), s, side)
+                cross = load(basis, (j, q ^ 2), s, side)
+                f = [
+                    made[part]
+                    + near[part]
+                    + high_fields[0] * x[1 - n][part]
+                    + high_fields[1] * cross[part]
+                    for part in range(2)
+                ]
+                dr = window(diagonal, (q, 0), side, s, 0)[...]
+                di = window(diagonal, (q, 1), side, s, 0)[...]
+                xr, xi = x[n]
+                w = (dr * xr - di * xi - f[0], dr * xi + di * xr - f[1])
+                more = pairing(x[n], w)
+                if before:
+                    more = more + pairing(load(basis, (j - 1, q), s, side), w)
+                if norm:
+                    more = more + (fold(w[0] * w[0] + w[1] * w[1]),)
+                for m, value in enumerate(more):
+                    acc[m] = acc[m] + value
+                for part in range(2):
+                    window(work, (slot, q), part, s, side)[...] = w[part]
+            if send and side == 1 and (s + 1) % (half // TILE) == 0:
+                work_copy(slot, 2 * pair + (s + 1) // (half // TILE) - 1).start()
+
+    def take(q, w_ref, u_ref, slot, now, before, after, coeffs, inverse, both, own):
+        for s, side in tiles:
+            rr, ri = load(w_ref, (slot, q), s, side)
+            for n, lead in enumerate([now, before] if both else [now]):
+                vr, vi = load(u_ref, (lead, q), s, side)
+                hr, hm = coeffs[2 * n], coeffs[2 * n + 1]
+                rr = rr - (hr * vr - hm * vi)
+                ri = ri - (hr * vi + hm * vr)
+            for part, value in enumerate((rr * inverse, ri * inverse)):
+                window(u_ref, (after, q), part, s, side)[...] = value
+                if own:
+                    put_split(q, part, s, side, value)
+
+    def apply(j, first, last):
+        slot = j % 2
+        acc = [zero_tile] * (2 + 2 * (not first) + (not last))
+        issue(2)
+        issue(3)
+        consume(j, 0, acc, not first, not last, not last)
+        if not first:
+            known = [scalars[j - 1, n] for n in range(6)]
+            for n in range(2, 4):
+                work_copy(1 - slot, n).wait()
+            for q in range(2, 4):
+                take(
+                    q, mate_work, mate, 1 - slot, 1 - slot, slot, slot, known[:4], known[5],
+                    True, False,
+                )
+        consume(j, 1, acc, not first, not last, False)
         return acc
 
-    def rest_inner(j):
+    def rest_inner(j, count):
         slot = j % 2
 
         def one(k, carry):
             def add(q, acc):
                 real, imag = acc
                 for s, side in tiles:
-                    wr = window(work, (slot, q), 0, s, side)[...]
-                    wi = window(work, (slot, q), 1, s, side)[...]
-                    more = inner(k, q, s, side, wr, wi)
+                    v = load(basis, (k, q), s, side)
+                    w = load(work, (slot, q), s, side)
+                    more = pairing(v, w)
                     real, imag = real + more[0], imag + more[1]
                 return real, imag
 
@@ -713,49 +752,40 @@
             own_rest[j, k, 1] = imag
             return carry
 
-        lax.fori_loop(0, j - 1, one, 0)
+        lax.fori_loop(0, count, one, 0)
 
     def step(j, first):
         slot = j % 2
-        against = [j] if first else [j, j - 1]
-        count = 2 * len(against) + 1
-        start_sums(apply(j, against, True), slot)
+        sums = apply(j, first, False)
+        start_sums(sums, slot)
+        for n in range(2, 4):
+            work_copy(slot, n).start()
         if not first:
-            rest_inner(j)
-        coeffs = finish_sums(count, slot)
+            rest_inner(j, j - 1)
+        coeffs = finish_sums(len(sums), slot)
         left = coeffs[-1]
         for value in coeffs[:-1]:
             left = left - value * value
         norm, inv_norm = scalar_sqrt(left)
-        for n, value in enumerate(coeffs[:-1]):
-            scalars[j, n] = value
+        for n in range(4):
+            scalars[j, n] = coeffs[n] if n < len(coeffs) - 1 else jnp.float32(0.0)
         scalars[j, 4] = norm
         scalars[j, 5] = inv_norm
-
-        def subtract(q, w_ref, u_ref, now, before, after):
-            for s, side in tiles:
-                rr = window(w_ref, (slot, q), 0, s, side)[...]
-                ri = window(w_ref, (slot, q), 1, s, side)[...]
-                for n, lead in enumerate([now] if first else [now, before]):
-                    vr = window(u_ref, (lead, q), 0, s, side)[...]
-                    vi = window(u_ref, (lead, q), 1, s, side)[...]
-                    hr, hm = coeffs[2 * n], coeffs[2 * n + 1]
-                    rr = rr - (hr * vr - hm * vi)
-                    ri = ri - (hr * vi + hm * vr)
-                window(u_ref, (after, q), 0, s, side)[...] = rr * inv_norm
-                window(u_ref, (after, q), 1, s, side)[...] = ri * inv_norm
-
-        subtract(0, work, basis, j, j - 1, j + 1)
-        issue(j + 1, 0)
-        for q in range(1, quarters):
-            subtract(q, work, basis, j, j - 1, j + 1)
+        for n in range(2):
+            work_copy(slot, n).wait()
         for q in range(quarters):
-            work_copy(slot, q).wait()
-        for q in range(quarters):
-            subtract(q, mate_work, mate, slot, 1 - slot, 1 - slot)
+            take(q, work, basis, slot, j, j - 1, j + 1, coeffs, inv_norm, not first, True)
+            if q < 2:
+                issue(q)
+        for q in range(2):
+            take(
+                q, mate_work, mate, slot, slot, 1 - slot, 1 - slot, coeffs, inv_norm,
+                not first, False,
+            )
 
     final = KRYLOV - 1
-    issue(0, 0)
+    issue(0)
+    issue(1)
     step(0, True)
 
     def later(j, carry):
@@ -763,9 +793,20 @@
         return carry
 
     lax.fori_loop(1, final, later, 0)
-    rest_copy = remote(own_rest, other_rest, rest_sem.at[0], rest_sem.at[1], other)
+    rest_copy = remote(
+        own_rest.at[pl.ds(0, final)],
+        other_rest.at[pl.ds(0, final)],
+        rest_sem.at[0],
+        rest_sem.at[1],
+        other,
+    )
+    last_copy = remote(
+        own_rest.at[final], other_rest.at[final], rest_sem.at[2], rest_sem.at[3], other
+    )
     rest_copy.start()
-    start_sums(apply(final, list(range(KRYLOV)), False), final % 2)
+    start_sums(apply(final, False, True), final % 2)
+    rest_inner(final, final - 1)
+    last_copy.start()
     rest_copy.wait()
     sub = lax.broadcasted_iota(jnp.int32, (8, LANES), 0)
     lane = lax.broadcasted_iota(jnp.int32, (8, LANES), 1)
@@ -805,7 +846,13 @@
         gram[1] = gram[1] + jnp.where(lane == j + 1, column[j + 1][1], 0.0)
         gram[1] = gram[1] - jnp.where(sub == j + 1, across[j + 1][1], 0.0)
 
-    targets = finish_sums(2 * KRYLOV, final % 2)
+    near_targets = finish_sums(4, final % 2)
+    last_copy.wait()
+    targets = []
+    for k in range(final - 1):
+        for part in range(2):
+            targets.append(jnp.sum(own_rest[final, k, part] + other_rest[final, k, part]))
+    targets = targets + near_targets[2:4] + near_targets[:2]
     for k in range(KRYLOV):
         for part in range(2):
             gram[part] = put(gram[part], (lane == KRYLOV) & (sub == k), targets[2 * k + part])
@@ -865,14 +912,14 @@
     ]
     channel_copy.wait()
     channel = jnp.where(stays, own_channel[...], other_channel[...])
-    sub_pos = lax.broadcasted_iota(jnp.int32, (SUB, LANES), 0) * LANES
-    sub_pos = sub_pos + lax.broadcasted_iota(jnp.int32, (SUB, LANES), 1)
+    sub_pos = lax.broadcasted_iota(jnp.int32, (TILE, LANES), 0) * LANES
+    sub_pos = sub_pos + lax.broadcasted_iota(jnp.int32, (TILE, LANES), 1)
 
     def combine(q, acc):
         high = (core << split_spin) + (q << (split_spin + 1))
         for s, side in tiles:
-            pr = jnp.zeros((SUB, LANES), jnp.float32)
-            pi = jnp.zeros((SUB, LANES), jnp.float32)
+            pr = jnp.zeros((TILE, LANES), jnp.float32)
+            pi = jnp.zeros((TILE, LANES), jnp.float32)
             for k in range(KRYLOV):
                 vr = window(basis, (k, q), 0, s, side)[...]
                 vi = window(basis, (k, q), 1, s, side)[...]
@@ -881,7 +928,7 @@
                 pi = pi + (cr * vi + ci * vr)
             window(work, (0, q), 0, s, side)[...] = pr
             window(work, (0, q), 1, s, side)[...] = pi
-            position = sub_pos + (high + (side << side_spin) + s * SUB * LANES)
+            position = sub_pos + (high + (side << side_spin) + s * TILE * LANES)
             occupied = lax.shift_right_logical(position, channel) & 1
             acc = acc + fold(jnp.where(occupied == 1, pr * pr + pi * pi, 0.0))
         return acc
@@ -896,7 +943,7 @@
             for b in range(SPINS - 1 - split_spin):
                 flipped = window(work, (0, q | (1 << b)), part, s, side)[...]
                 value = jnp.where(channel == split_spin + 1 + b, flipped, value)
-            target[s * SUB : (s + 1) * SUB, side * LANES : (side + 1) * LANES] = value
+            target[s * TILE : (s + 1) * TILE, side * LANES : (side + 1) * LANES] = value
 
     parcels = []
     for part in range(2):
@@ -1031,18 +1078,18 @@
             pltpu.VMEM((2, quarters, 2, BLOCK, BLOCK), f32),
             pltpu.VMEM((2, quarters, 2, BLOCK, BLOCK), f32),
             pltpu.VMEM((2, quarters, 2, BLOCK, BLOCK), f32),
-            pltpu.VMEM((2, BLOCK, BLOCK), f32),
-            pltpu.VMEM((2, BLOCK, BLOCK), f32),
+            pltpu.VMEM((quarters, 2, BLOCK, BLOCK), f32),
+            pltpu.VMEM((quarters, 2, 2, BLOCK, BLOCK), jnp.bfloat16),
             pltpu.VMEM((BLOCK, 3 * BLOCK), jnp.bfloat16),
             pltpu.VMEM((3 * BLOCK, BLOCK), jnp.bfloat16),
             pltpu.VMEM((quarters, 2, 2, BLOCK, LANES), f32),
             pltpu.VMEM((2, sums_rows, LANES), f32),
             pltpu.VMEM((2, sums_rows, LANES), f32),
-            pltpu.VMEM((KRYLOV - 1, KRYLOV - 3, 2, 8, LANES), f32),
-            pltpu.VMEM((KRYLOV - 1, KRYLOV - 3, 2, 8, LANES), f32),
+            pltpu.VMEM((KRYLOV, KRYLOV - 2, 2, 8, LANES), f32),
+            pltpu.VMEM((KRYLOV, KRYLOV - 2, 2, 8, LANES), f32),
             pltpu.SMEM((KRYLOV - 1, 6), f32),
-            pltpu.VMEM((SUB, LANES), jnp.int32),
-            pltpu.VMEM((SUB, LANES), jnp.int32),
+            pltpu.VMEM((TILE, LANES), jnp.int32),
+            pltpu.VMEM((TILE, LANES), jnp.int32),
             pltpu.VMEM((4, BLOCK, BLOCK), f32),
             dma((4,)),
             dma((quarters,)),
@@ -1050,7 +1097,7 @@
             dma((quarters,)),
             dma((2,)),
             dma((2,)),
-            dma((2,)),
+            dma((4,)),
             dma((2, quarters)),
             dma((2, quarters)),
             dma((2,)),

time: 106 us -> 98.4 us (0.928)
  Pallas kernels: 105 us -> 97.5 us
    pallas_call x1, Pallas kernels: 102 us -> 94 us  [paired_body(): pl.pallas_call(pair_kernel, out_shape=(jax.ShapeDtypeStruct((2, 2, BLOCK,...]
where the time goes in v3:
time: 98.4 us; the launch traced here: 98.2 us
  Pallas kernels  97.5 us (99%)
    pallas_call x1, Pallas kernels, paired_body(): pl.pallas_call(pair_kernel, out_shape=(jax.ShapeDtypeStruct((2, 2, BLOCK,...  94 us
    pallas_call x1, Pallas kernels, paired_body(): pl.pallas_call(lower_kernel, out_shape=jax.ShapeDtypeStruct((2 * block_ro...  3.59 us

profile of v3, /device:TPU:1, one launch (start us, length us, event | category | flops | bytes accessed | tf_op | source)
XLA Modules:
  0.0 98.2 jit_solution(11088253298535036322)
XLA Ops:
  0.7 94.0 %pair.1 = (f32[2,2,256,256]{3,2,1,0:T(8,128)}, f32[8,128]{1,0:T(8,128)}) custom-call(s32[1]{0:T(128)S(6)} %copy.8.channel_ref, f32[18]{0:T(128)} %couplings.1, f32[19]{0:T(128)} %fields.1, f32[19]{0:T(128)} %decays.1, f32[2048,128]{1,0:T(8,128)} %bitcast.10), custom_call_target="tpu_custom_call" | custom-call | tf_op jit(solution)/shard_map/pair/pallas_call | solution.py:1066
  94.6 3.6 %lower.1 = f32[2048,128]{1,0:T(8,128)} custom-call(s32[1]{0:T(128)S(6)} %copy.8.channel_ref, f32[2,2,256,256]{3,2,1,0:T(8,128)} %get-tuple-element.7.pieces, f32[8,128]{1,0:T(8,128)} %get-tuple-element.8.scale), custom_call_target="tpu_custom_call" | custom-call | tf_op jit(solution)/shard_map/lower/pallas_call | solution.py:1113

commit v4 on v3

--- a/solution.py
+++ b/solution.py
@@ -657,13 +657,12 @@
 
     high_fields = [fields[split_spin + 1 + b] * inv_unit for b in range(SPINS - 1 - split_spin)]
 
-    def issue(q):
-        for part in range(2):
-            hi, lo = splits[q, part, 0], splits[q, part, 1]
-            flips[q, part] = dot(
-                jnp.concatenate([row_table[...], hi, lo, hi], axis=1),
-                jnp.concatenate([hi, lo, hi, lane_table[...]], axis=0),
-            )
+    def issue(q, part):
+        hi, lo = splits[q, part, 0], splits[q, part, 1]
+        flips[q, part] = dot(
+            jnp.concatenate([row_table[...], hi, lo, hi], axis=1),
+            jnp.concatenate([hi, lo, hi, lane_table[...]], axis=0),
+        )
 
     def pairing(v, w):
         return fold(v[0] * w[0] + v[1] * w[1]), fold(v[0] * w[1] - v[1] * w[0])
@@ -671,9 +670,11 @@
     def load(ref, lead, s, side):
         return [window(ref, lead, part, s, side)[...] for part in range(2)]
 
-    def consume(j, pair, acc, before, norm, send):
+    def consume(j, pair, acc, before, norm, send, between=()):
         slot = j % 2
-        for s, side in tiles:
+        for t, (s, side) in enumerate(tiles):
+            if t % 8 == 0 and between:
+                issue(*between[t // 8])
             chosen = (2 * pair, 2 * pair + 1)
             x = [load(basis, (j, q), s, side) for q in chosen]
             for n, q in enumerate(chosen):
@@ -703,8 +704,10 @@
             if send and side == 1 and (s + 1) % (half // TILE) == 0:
                 work_copy(slot, 2 * pair + (s + 1) // (half // TILE) - 1).start()
 
-    def take(q, w_ref, u_ref, slot, now, before, after, coeffs, inverse, both, own):
-        for s, side in tiles:
+    def take(q, w_ref, u_ref, slot, now, before, after, coeffs, inverse, both, own, between=()):
+        for t, (s, side) in enumerate(tiles):
+            if t % 16 == 0 and between:
+                issue(*between[t // 16])
             rr, ri = load(w_ref, (slot, q), s, side)
             for n, lead in enumerate([now, before] if both else [now]):
                 vr, vi = load(u_ref, (lead, q), s, side)
@@ -719,13 +722,13 @@
     def apply(j, first, last):
         slot = j % 2
         acc = [zero_tile] * (2 + 2 * (not first) + (not last))
-        issue(2)
-        issue(3)
-        consume(j, 0, acc, not first, not last, not last)
         if not first:
             known = [scalars[j - 1, n] for n in range(6)]
             for n in range(2, 4):
                 work_copy(1 - slot, n).wait()
+        products = [(q, part) for q in (2, 3) for part in range(2)]
+        consume(j, 0, acc, not first, not last, not last, products)
+        if not first:
             for q in range(2, 4):
                 take(
                     q, mate_work, mate, 1 - slot, 1 - slot, slot, slot, known[:4], known[5],
@@ -774,9 +777,10 @@
         for n in range(2):
             work_copy(slot, n).wait()
         for q in range(quarters):
-            take(q, work, basis, slot, j, j - 1, j + 1, coeffs, inv_norm, not first, True)
-            if q < 2:
-                issue(q)
+            between = [(q - 1, part) for part in range(2)] if 0 < q < 3 else ()
+            take(
+                q, work, basis, slot, j, j - 1, j + 1, coeffs, inv_norm, not first, True, between
+            )
         for q in range(2):
             take(
                 q, mate_work, mate, slot, slot, 1 - slot, 1 - slot, coeffs, inv_norm,
@@ -784,8 +788,9 @@
             )
 
     final = KRYLOV - 1
-    issue(0)
-    issue(1)
+    for q in range(2):
+        for part in range(2):
+            issue(q, part)
     step(0, True)
 
     def later(j, carry):
@@ -1106,7 +1111,7 @@
             dma((2,)),
         ],
         compiler_params=pltpu.CompilerParams(
-            collective_id=1, has_side_effects=True, vmem_limit_bytes=62 * 1024 * 1024
+            collective_id=1, has_side_effects=True, vmem_limit_bytes=48 * 1024 * 1024
         ),
         name="pair",
     )(channel, couplings, fields, decays, state)
@@ -1115,6 +1120,7 @@
         out_shape=jax.ShapeDtypeStruct((2 * block_rows, LANES), f32),
         in_specs=[smem, vmem, vmem],
         out_specs=vmem,
+        compiler_params=pltpu.CompilerParams(vmem_limit_bytes=8 * 1024 * 1024),
         name="lower",
     )(channel, pieces, scale)
     lowered = lowered.reshape(block_rows, 2, LANES).transpose(1, 0, 2)

time: 98.4 us -> 95.5 us (0.971)
  Pallas kernels: 97.5 us -> 92.7 us
  local copies, waits for them, and re-layouts: 0 us -> 1.89 us
    pallas_call x1, Pallas kernels: 94 us -> 90.3 us  [paired_body(): pl.pallas_call(pair_kernel, out_shape=(jax.ShapeDtypeStruct((2, 2, BLOCK,...]
    unnamed x0 -> x8, local copies, waits for them, and re-layouts: none -> 1.89 us
    pallas_call x1, Pallas kernels: 3.59 us -> 2.38 us  [paired_body(): pl.pallas_call(lower_kernel, out_shape=jax.ShapeDtypeStruct((2 * block_ro...]
where the time goes in v4:
time: 95.5 us; the launch traced here: 95.3 us
  Pallas kernels  92.7 us (97%)
  local copies, waits for them, and re-layouts  1.89 us (2%)
    pallas_call x1, Pallas kernels, paired_body(): pl.pallas_call(pair_kernel, out_shape=(jax.ShapeDtypeStruct((2, 2, BLOCK,...  90.3 us
    pallas_call x1, Pallas kernels, paired_body(): pl.pallas_call(lower_kernel, out_shape=jax.ShapeDtypeStruct((2 * block_ro...  2.38 us

profile of v4, /device:TPU:1, one launch (start us, length us, event | category | flops | bytes accessed | tf_op | source)
XLA Modules:
  0.0 95.3 jit_solution(8745724444794757289)
XLA Ops:
  0.7 0.0 copy-start.1
  0.7 0.0 copy-start.2
  0.7 0.0 copy-start.3
  0.7 0.6 copy-done.1
  1.3 0.0 copy-done.2
  1.3 0.0 copy-done.3
  1.3 0.0 copy-start
  1.3 1.2 %copy-done = f32[1,2,131072]{2,1,0:T(2,128)S(1)} copy-done((f32[1,2,131072]{2,1,0:T(2,128)S(1)}, f32[1,2,131072]{2,1,0:T(2,128)}, u32[]{:S(2)}) %copy-start) | copy-done | bytes 1048600
  2.6 90.3 %pair.1 = (f32[2,2,256,256]{3,2,1,0:T(8,128)S(1)}, f32[8,128]{1,0:T(8,128)S(1)}) custom-call(s32[1]{0:T(128)S(6)} %copy.8.channel_ref, f32[18]{0:T(128)S(1)} %copy-done.1, f32[19]{0:T(128)S(1)} %copy-done.2, f32[19]{0:T(128)S(1)} %copy-done.3, f32[2048,128]{1,0:T(8,128)S(1)} %bitcast.10), custom_call_target="tpu_custom_call" | custom-call | tf_op jit(solution)/shard_map/pair/pallas_call | solution.py:1071
  92.9 2.4 %lower.1 = f32[2048,128]{1,0:T(8,128)} custom-call(s32[1]{0:T(128)S(6)} %copy.8.channel_ref, f32[2,2,256,256]{3,2,1,0:T(8,128)S(1)} %get-tuple-element.7.pieces, f32[8,128]{1,0:T(8,128)S(1)} %get-tuple-element.8.scale), custom_call_target="tpu_custom_call" | custom-call | tf_op jit(solution)/shard_map/lower/pallas_call | solution.py:1118
Async XLA Ops:
  0.7 0.7 copy-start.1
  0.7 0.7 copy-start.2
  0.7 0.7 copy-start.3
  1.3 1.2 %copy-start = (f32[1,2,131072]{2,1,0:T(2,128)S(1)}, f32[1,2,131072]{2,1,0:T(2,128)}, u32[]{:S(2)}) copy-start(f32[1,2,131072]{2,1,0:T(2,128)} %param.5) | copy-start | bytes 3145732

commit v5 on v4

--- a/solution.py
+++ b/solution.py
@@ -670,9 +670,9 @@
     def load(ref, lead, s, side):
         return [window(ref, lead, part, s, side)[...] for part in range(2)]
 
-    def consume(j, pair, acc, before, norm, send, between=()):
-        slot = j % 2
-        for t, (s, side) in enumerate(tiles):
+    def consume(j, slot, pair, acc, before, norm, h, between=()):
+        count = len(tiles) // 2
+        for t, (s, side) in enumerate(tiles[h * count : (h + 1) * count]):
             if t % 8 == 0 and between:
                 issue(*between[t // 8])
             chosen = (2 * pair, 2 * pair + 1)
@@ -701,44 +701,55 @@
                     acc[m] = acc[m] + value
                 for part in range(2):
                     window(work, (slot, q), part, s, side)[...] = w[part]
-            if send and side == 1 and (s + 1) % (half // TILE) == 0:
-                work_copy(slot, 2 * pair + (s + 1) // (half // TILE) - 1).start()
 
     def take(q, w_ref, u_ref, slot, now, before, after, coeffs, inverse, both, own, between=()):
-        for t, (s, side) in enumerate(tiles):
+        group = 4
+        leads = [now, before] if both else [now]
+        for t in range(0, len(tiles), group):
             if t % 16 == 0 and between:
                 issue(*between[t // 16])
-            rr, ri = load(w_ref, (slot, q), s, side)
-            for n, lead in enumerate([now, before] if both else [now]):
-                vr, vi = load(u_ref, (lead, q), s, side)
-                hr, hm = coeffs[2 * n], coeffs[2 * n + 1]
-                rr = rr - (hr * vr - hm * vi)
-                ri = ri - (hr * vi + hm * vr)
-            for part, value in enumerate((rr * inverse, ri * inverse)):
-                window(u_ref, (after, q), part, s, side)[...] = value
-                if own:
-                    put_split(q, part, s, side, value)
-
-    def apply(j, first, last):
-        slot = j % 2
+            made = []
+            for s, side in tiles[t : t + group]:
+                rr, ri = load(w_ref, (slot, q), s, side)
+                vs = [load(u_ref, (lead, q), s, side) for lead in leads]
+                made.append((rr, ri, vs))
+            for (s, side), (rr, ri, vs) in zip(tiles[t : t + group], made):
+                for n, (vr, vi) in enumerate(vs):
+                    hr, hm = coeffs[2 * n], coeffs[2 * n + 1]
+                    rr = rr - (hr * vr - hm * vi)
+                    ri = ri - (hr * vi + hm * vr)
+                for part, value in enumerate((rr * inverse, ri * inverse)):
+                    window(u_ref, (after, q), part, s, side)[...] = value
+                    if own:
+                        put_split(q, part, s, side, value)
+
+    def apply(j, slot, first, last):
         acc = [zero_tile] * (2 + 2 * (not first) + (not last))
+        middle = None
         if not first:
             known = [scalars[j - 1, n] for n in range(6)]
             for n in range(2, 4):
                 work_copy(1 - slot, n).wait()
-        products = [(q, part) for q in (2, 3) for part in range(2)]
-        consume(j, 0, acc, not first, not last, not last, products)
-        if not first:
-            for q in range(2, 4):
+
+            def middle(q):
                 take(
                     q, mate_work, mate, 1 - slot, 1 - slot, slot, slot, known[:4], known[5],
                     True, False,
                 )
-        consume(j, 1, acc, not first, not last, False)
+
+        for h in range(2):
+            products = [(2 + h, part) for part in range(2)]
+            consume(j, slot, 0, acc, not first, not last, h, products)
+            if not last:
+                work_copy(slot, h).start()
+        if middle:
+            middle(2)
+            middle(3)
+        for h in range(2):
+            consume(j, slot, 1, acc, not first, not last, h)
         return acc
 
-    def rest_inner(j, count):
-        slot = j % 2
+    def rest_inner(j, slot, count):
 
         def one(k, carry):
             def add(q, acc):
@@ -757,14 +768,13 @@
 
         lax.fori_loop(0, count, one, 0)
 
-    def step(j, first):
-        slot = j % 2
-        sums = apply(j, first, False)
+    def step(j, slot, first):
+        sums = apply(j, slot, first, False)
         start_sums(sums, slot)
         for n in range(2, 4):
             work_copy(slot, n).start()
         if not first:
-            rest_inner(j, j - 1)
+            rest_inner(j, slot, j - 1)
         coeffs = finish_sums(len(sums), slot)
         left = coeffs[-1]
         for value in coeffs[:-1]:
@@ -774,10 +784,11 @@
             scalars[j, n] = coeffs[n] if n < len(coeffs) - 1 else jnp.float32(0.0)
         scalars[j, 4] = norm
         scalars[j, 5] = inv_norm
-        for n in range(2):
-            work_copy(slot, n).wait()
         for q in range(quarters):
-            between = [(q - 1, part) for part in range(2)] if 0 < q < 3 else ()
+            if q == 2:
+                for n in range(2):
+                    work_copy(slot, n).wait()
+            between = [(q - 2, part) for part in range(2)] if q > 1 else ()
             take(
                 q, work, basis, slot, j, j - 1, j + 1, coeffs, inv_norm, not first, True, between
             )
@@ -791,13 +802,14 @@
     for q in range(2):
         for part in range(2):
             issue(q, part)
-    step(0, True)
-
-    def later(j, carry):
-        step(j, False)
+    step(0, 0, True)
+
+    def later(i, carry):
+        step(2 * i + 1, 1, False)
+        step(2 * i + 2, 0, False)
         return carry
 
-    lax.fori_loop(1, final, later, 0)
+    lax.fori_loop(0, final // 2, later, 0)
     rest_copy = remote(
         own_rest.at[pl.ds(0, final)],
         other_rest.at[pl.ds(0, final)],
@@ -809,8 +821,8 @@
         own_rest.at[final], other_rest.at[final], rest_sem.at[2], rest_sem.at[3], other
     )
     rest_copy.start()
-    start_sums(apply(final, False, True), final % 2)
-    rest_inner(final, final - 1)
+    start_sums(apply(final, final % 2, False, True), final % 2)
+    rest_inner(final, final % 2, final - 1)
     last_copy.start()
     rest_copy.wait()
     sub = lax.broadcasted_iota(jnp.int32, (8, LANES), 0)

time: 95.5 us -> 90.5 us (0.948)
  Pallas kernels: 92.7 us -> 87.8 us
    pallas_call x1, Pallas kernels: 90.3 us -> 85.4 us  [paired_body(): pl.pallas_call(pair_kernel, out_shape=(jax.ShapeDtypeStruct((2, 2, BLOCK,...]
where the time goes in v5:
time: 90.5 us; the launch traced here: 90.3 us
  Pallas kernels  87.8 us (97%)
  local copies, waits for them, and re-layouts  1.89 us (2%)
    pallas_call x1, Pallas kernels, paired_body(): pl.pallas_call(pair_kernel, out_shape=(jax.ShapeDtypeStruct((2, 2, BLOCK,...  85.4 us
    pallas_call x1, Pallas kernels, paired_body(): pl.pallas_call(lower_kernel, out_shape=jax.ShapeDtypeStruct((2 * block_ro...  2.38 us
    unnamed x8, local copies, waits for them, and re-layouts  1.89 us

profile of v5, /device:TPU:1, one launch (start us, length us, event | category | flops | bytes accessed | tf_op | source)
XLA Modules:
  0.0 90.3 jit_solution(7533541171841757164)
XLA Ops:
  0.7 0.0 copy-start.1
  0.7 0.0 copy-start.2
  0.7 0.0 copy-start.3
  0.7 0.6 copy-done.1
  1.3 0.0 copy-done.2
  1.3 0.0 copy-done.3
  1.3 0.0 copy-start
  1.3 1.2 %copy-done = f32[1,2,131072]{2,1,0:T(2,128)S(1)} copy-done((f32[1,2,131072]{2,1,0:T(2,128)S(1)}, f32[1,2,131072]{2,1,0:T(2,128)}, u32[]{:S(2)}) %copy-start) | copy-done | bytes 1048600
  2.6 85.4 %pair.1 = (f32[2,2,256,256]{3,2,1,0:T(8,128)S(1)}, f32[8,128]{1,0:T(8,128)S(1)}) custom-call(s32[1]{0:T(128)S(6)} %copy.8.channel_ref, f32[18]{0:T(128)S(1)} %copy-done.1, f32[19]{0:T(128)S(1)} %copy-done.2, f32[19]{0:T(128)S(1)} %copy-done.3, f32[2048,128]{1,0:T(8,128)S(1)} %bitcast.10), custom_call_target="tpu_custom_call" | custom-call | tf_op jit(solution)/shard_map/pair/pallas_call | solution.py:1083
  88.0 2.4 %lower.1 = f32[2048,128]{1,0:T(8,128)} custom-call(s32[1]{0:T(128)S(6)} %copy.8.channel_ref, f32[2,2,256,256]{3,2,1,0:T(8,128)S(1)} %get-tuple-element.7.pieces, f32[8,128]{1,0:T(8,128)S(1)} %get-tuple-element.8.scale), custom_call_target="tpu_custom_call" | custom-call | tf_op jit(solution)/shard_map/lower/pallas_call | solution.py:1130
Async XLA Ops:
  0.7 0.7 copy-start.1
  0.7 0.7 copy-start.2
  0.7 0.7 copy-start.3
  1.3 1.2 %copy-start = (f32[1,2,131072]{2,1,0:T(2,128)S(1)}, f32[1,2,131072]{2,1,0:T(2,128)}, u32[]{:S(2)}) copy-start(f32[1,2,131072]{2,1,0:T(2,128)} %param.5) | copy-start | bytes 3145732

commit v6 on v5

--- a/solution.py
+++ b/solution.py
@@ -728,8 +728,6 @@
         middle = None
         if not first:
             known = [scalars[j - 1, n] for n in range(6)]
-            for n in range(2, 4):
-                work_copy(1 - slot, n).wait()
 
             def middle(q):
                 take(
@@ -743,6 +741,8 @@
             if not last:
                 work_copy(slot, h).start()
         if middle:
+            for n in range(2, 4):
+                work_copy(1 - slot, n).wait()
             middle(2)
             middle(3)
         for h in range(2):

time: 90.5 us -> 92.7 us (1.024)
  Pallas kernels: 87.8 us -> 90 us
    pallas_call x1, Pallas kernels: 85.4 us -> 87.6 us  [paired_body(): pl.pallas_call(pair_kernel, out_shape=(jax.ShapeDtypeStruct((2, 2, BLOCK,...]
where the time goes in v6:
time: 92.7 us; the launch traced here: 92.6 us
  Pallas kernels  90 us (97%)
  local copies, waits for them, and re-layouts  1.89 us (2%)
    pallas_call x1, Pallas kernels, paired_body(): pl.pallas_call(pair_kernel, out_shape=(jax.ShapeDtypeStruct((2, 2, BLOCK,...  87.6 us
    pallas_call x1, Pallas kernels, paired_body(): pl.pallas_call(lower_kernel, out_shape=jax.ShapeDtypeStruct((2 * block_ro...  2.38 us
    unnamed x8, local copies, waits for them, and re-layouts  1.89 us

profile of v6, /device:TPU:1, one launch (start us, length us, event | category | flops | bytes accessed | tf_op | source)
XLA Modules:
  0.0 92.6 jit_solution(6280043674217667665)
XLA Ops:
  0.7 0.0 copy-start.1
  0.7 0.0 copy-start.2
  0.7 0.0 copy-start.3
  0.7 0.6 copy-done.1
  1.3 0.0 copy-done.2
  1.3 0.0 copy-done.3
  1.3 0.0 copy-start
  1.3 1.2 %copy-done = f32[1,2,131072]{2,1,0:T(2,128)S(1)} copy-done((f32[1,2,131072]{2,1,0:T(2,128)S(1)}, f32[1,2,131072]{2,1,0:T(2,128)}, u32[]{:S(2)}) %copy-start) | copy-done | bytes 1048600
  2.6 87.6 %pair.1 = (f32[2,2,256,256]{3,2,1,0:T(8,128)S(1)}, f32[8,128]{1,0:T(8,128)S(1)}) custom-call(s32[1]{0:T(128)S(6)} %copy.8.channel_ref, f32[18]{0:T(128)S(1)} %copy-done.1, f32[19]{0:T(128)S(1)} %copy-done.2, f32[19]{0:T(128)S(1)} %copy-done.3, f32[2048,128]{1,0:T(8,128)S(1)} %bitcast.10), custom_call_target="tpu_custom_call" | custom-call | tf_op jit(solution)/shard_map/pair/pallas_call | solution.py:1083
  90.2 2.4 %lower.1 = f32[2048,128]{1,0:T(8,128)} custom-call(s32[1]{0:T(128)S(6)} %copy.8.channel_ref, f32[2,2,256,256]{3,2,1,0:T(8,128)S(1)} %get-tuple-element.7.pieces, f32[8,128]{1,0:T(8,128)S(1)} %get-tuple-element.8.scale), custom_call_target="tpu_custom_call" | custom-call | tf_op jit(solution)/shard_map/lower/pallas_call | solution.py:1130
Async XLA Ops:
  0.7 0.7 copy-start.1
  0.7 0.7 copy-start.2
  0.7 0.7 copy-start.3
  1.3 1.2 %copy-start = (f32[1,2,131072]{2,1,0:T(2,128)S(1)}, f32[1,2,131072]{2,1,0:T(2,128)}, u32[]{:S(2)}) copy-start(f32[1,2,131072]{2,1,0:T(2,128)} %param.5) | copy-start | bytes 3145732
